TPU v7x, 128 devices: a whole 4x4x4 slice. The times are simulated.
128 devices in a mesh: pipe: 2 (over x_lo), tensor: 4 (over x_hi, core), dp: 16 (over z, y).
Axes of the slice: x: 4 (x_hi: 2, x_lo: 2; x = x_hi * 2 + x_lo), y: 4, z: 4, core: 2. Of those that a mesh axis runs over, the one named last changes fastest.
Arguments:
- inputs: bfloat16 [2, 2048, 16384], P(None, 'dp', 'tensor'), may hold values from -6 to 6
- w_in: bfloat16 [2, 16384, 1024], P('pipe', ('tensor', 'dp')), may hold values from -0.046875 to 0.046875
- w_out: bfloat16 [2, 1024, 16384], P('pipe', None, ('tensor', 'dp')), may hold values from -0.1875 to 0.1875
- cotangent: bfloat16 [2, 2048, 16384], P(None, 'dp', 'tensor'), may hold values from -6 to 6
Outputs:
- update_in: float32 [2, 16384, 1024], P('pipe', ('tensor', 'dp'))
- update_out: float32 [2, 1024, 16384], P('pipe', None, ('tensor', 'dp'))
- grad_norm: float32 [], replicated
All inputs are finite; a program needn't handle non-finite values.
Results may differ from a plain program's by a relative error of at most 0.008.
Values may be sent and summed in bfloat16 or wider, within the bound.
No kernel may reach another device: no remote copies, remote signals or barrier semaphores. Data moves between devices by JAX's collectives and lax.ppermute only.
A program may use at most 192 MiB of HBM per device.

v0:
```python
import functools

import jax
import jax.numpy as jnp
from jax import lax
from jax.experimental import pallas as pl
from jax.experimental.pallas import tpu as pltpu
from jax.sharding import Mesh
from jax.sharding import PartitionSpec as P


CLIP_NORM = 16384
AXES = ("p", "h", "c", "z", "y")
BF = jnp.bfloat16
F32 = jnp.float32


def dot(a, b):
    return jnp.dot(a, b, preferred_element_type=F32)


def dot_t0(a, b):
    return lax.dot_general(a, b, (((0,), (0,)), ((), ())), preferred_element_type=F32)


def dot_t1(a, b):
    return lax.dot_general(a, b, (((1,), (1,)), ((), ())), preferred_element_type=F32)


def a2a(value, axes):
    return lax.all_to_all(value, axes, 0, 0, tiled=True)


def shift(value, axis, by):
    count = lax.axis_size(axis)
    return lax.ppermute(value, axis, [(i, (i + by) % count) for i in range(count)])


def shift_x(value, by):
    pairs = []
    for p in range(2):
        for h in range(2):
            to = (h * 2 + p + by) % 4
            pairs.append((p * 2 + h, (to % 2) * 2 + to // 2))
    return lax.ppermute(value, ("p", "h"), pairs)


def silu_bf(pre):
    return jax.nn.silu(pre).astype(BF)


def slope_bf(up, pre):
    s = jax.nn.sigmoid(pre)
    return (up * s * (1.0 + pre * (1.0 - s))).astype(BF)


def cut_kernel(along_z, at_ref, one_ref, two_ref, *outs):
    p, x, c, z, y = (at_ref[i] for i in range(5))
    tok = one_ref.shape[0]
    own = one_ref.shape[1] // 16
    half, part = tok // 2, tok // 8
    for rc in range(2):
        for q in range(4):
            source = lax.rem(c + rc, 2) * half + lax.rem(x + 4 - q, 4) * part
            rows = pl.ds(pl.multiple_of(source, part), part)
            to = rc * half + q * part
            for k in range(4):
                for j in range(4):
                    if along_z:
                        zz, yy = lax.rem(z + k, 4), lax.rem(y + 4 - j, 4)
                    else:
                        zz, yy = lax.rem(z + 4 - j, 4), lax.rem(y + k, 4)
                    cols = pl.ds(pl.multiple_of((zz * 4 + yy) * own, own), own)
                    got = jnp.where(p == 0, one_ref[rows, cols], two_ref[rows, cols])
                    outs[k][to : to + part, j * own : (j + 1) * own] = got


def cut(at, one, two, along_z):
    tok, width = one.shape
    vmem = pl.BlockSpec(memory_space=pltpu.VMEM)
    return pl.pallas_call(
        functools.partial(cut_kernel, along_z),
        out_shape=[jax.ShapeDtypeStruct((tok, width // 4), BF)] * 4,
        in_specs=[pl.BlockSpec(memory_space=pltpu.SMEM), vmem, vmem],
        out_specs=[vmem] * 4,
        name="cut_z" if along_z else "cut_y",
    )(at, one, two)


def project_kernel(*refs):
    blocks, weights, sent, kept = refs[:4], refs[4:8], refs[8], refs[9]
    half = blocks[0].shape[0] // 2
    own = weights[0].shape[0]
    for rc, out in ((1, sent), (0, kept)):
        left = jnp.concatenate([b[rc * half : (rc + 1) * half, :] for b in blocks])
        total = dot(left[:, :own], weights[0][...])
        for j in range(1, 4):
            total += dot(left[:, j * own : (j + 1) * own], weights[j][...])
        out[...] = total.astype(out.dtype)


def project(blocks, weights):
    tok, wide = blocks[0].shape
    own, hidden = weights[0].shape
    tile = hidden // 4
    return pl.pallas_call(
        project_kernel,
        out_shape=[
            jax.ShapeDtypeStruct((2 * tok, hidden), BF),
            jax.ShapeDtypeStruct((2 * tok, hidden), F32),
        ],
        grid=(4,),
        in_specs=[pl.BlockSpec((tok, wide), lambda n: (0, 0))] * 4
        + [pl.BlockSpec((own, tile), lambda n: (0, n))] * 4,
        out_specs=[pl.BlockSpec((2 * tok, tile), lambda n: (0, n))] * 2,
        cost_estimate=pl.CostEstimate(
            flops=8 * tok * wide * hidden, bytes_accessed=8 * tok * wide * 2, transcendentals=0
        ),
    )(*blocks, *weights)


def store_piece(outs, j, total):
    for i in range(4):

        @pl.when(j == i)
        def _(i=i):
            outs[i][...] = total.astype(outs[i].dtype)


def grad_v_kernel(*refs):
    blocks, near, far, outs = refs[:4], refs[4:8], refs[8:12], refs[12:]
    total = None
    for k in range(4):
        right = jnp.concatenate([near[k][...], far[k][...]])
        term = dot_t0(blocks[k][...], right)
        total = term if total is None else total + term
    store_piece(outs, pl.program_id(0), total)


def grad_u_kernel(*refs):
    blocks, near, far = refs[:4], refs[4:8], refs[8:12]
    w_ref, outs = refs[12], refs[13:]
    total = None
    for k in range(4):
        right = jnp.concatenate([near[k][0], far[k][0]])
        factor = jnp.concatenate([near[k][1], far[k][1]])
        left = blocks[k][...].astype(F32) + dot_t1(factor, w_ref[...])
        term = dot_t0(left.astype(BF), right)
        total = term if total is None else total + term
    store_piece(outs, pl.program_id(0), total)


def gradient(kernel, blocks, near, far, weights):
    tok, wide = blocks[0].shape
    own = wide // 4
    hidden = near[0].shape[-1]

    def whole(a):
        return pl.BlockSpec(a.shape, lambda j: (0,) * a.ndim)

    def piece(dtype):
        return jax.ShapeDtypeStruct((own, hidden), dtype)

    fold = [pl.BlockSpec((own, hidden), lambda j: (j, 0))] * len(weights)
    return pl.pallas_call(
        kernel,
        out_shape=[piece(F32)] + [piece(BF)] * 3,
        grid=(4,),
        in_specs=[pl.BlockSpec((tok, own), lambda j: (0, j))] * 4
        + [whole(a) for a in (*near, *far)]
        + fold,
        out_specs=[pl.BlockSpec((own, hidden), lambda j: (0, 0))] * 4,
        cost_estimate=pl.CostEstimate(
            flops=8 * tok * wide * hidden, bytes_accessed=8 * tok * wide * 2, transcendentals=0
        ),
    )(*blocks, *near, *far, *weights)


def gather(value, axis):
    return [value] + [shift(value, axis, k) for k in (1, 2, 3)]


def exchange(pieces, axis, sign):
    return [pieces[0]] + [shift(pieces[k], axis, sign * k) for k in (1, 2, 3)]


def sum_back(blocks, axis):
    parts = exchange([blocks[0]] + [b.astype(BF) for b in blocks[1:]], axis, -1)
    return sum((part.astype(F32) for part in parts[1:]), parts[0])


def on_device(inputs, w_in, w_out, cotangent):
    p, h, c, z, y = (lax.axis_index(a) for a in AXES)
    first = p == 0
    n_micro, rows, cols = inputs.shape
    tok = n_micro * rows
    hidden = w_in.shape[2]
    half = tok // 2
    mine = half // 4

    w_i = w_in[0]
    w_o = w_out[0].T
    w_u = jnp.where(first, w_o, w_i)
    w_v = jnp.where(first, w_i, w_o)
    w_3 = lax.ppermute(w_u, "p", [(0, 1), (1, 0)])
    w_vs = gather(w_v, "y")
    at = jnp.stack([p, h * 2 + p, c, z, y])
    x = inputs.reshape(tok, cols)
    ct = cotangent.reshape(tok, cols)
    vs = list(cut(at, x, ct, True))
    us = list(cut(at, ct, x, False))
    vs[0], us[0], w_3 = lax.optimization_barrier((vs[0], us[0], w_3))
    vs = exchange(vs, "z", 1)
    us = exchange(us, "y", 1)
    w_us = gather(w_u, "z")

    m = dot_t0(jnp.where(first, w_u, w_3), jnp.where(first, w_3, w_u))
    m = lax.dynamic_index_in_dim(m.reshape(2, 16, 2, 2, -1, hidden), p, 2, False)
    m = m.transpose(1, 2, 0, 3, 4).reshape(hidden // 2, hidden).astype(BF)
    m = a2a(m, ("z", "y", "h", "c")).reshape(64, -1, hidden)
    m = m.astype(F32).sum(0).astype(BF)
    m = a2a(jnp.broadcast_to(m[None], (4,) + m.shape), ("p", "h")).reshape(-1, hidden)
    w_us[0], m = lax.optimization_barrier((w_us[0], m))
    m_near = lax.all_gather(m, ("z", "y"), axis=0, tiled=True)
    m_far = shift(m_near, "c", 1)

    def reduced(blocks, weights, axis):
        sent, kept = project(blocks, weights)
        kept = kept + shift(sent, "c", 1).astype(F32)
        return sum_back([kept[k * half : (k + 1) * half] for k in range(4)], axis)

    a_v = reduced(vs, w_vs, "z")
    a_u = reduced(us, w_us, "y")
    a_u, a_v, w_3 = lax.optimization_barrier((a_u, a_v, w_3))
    w_3 = jnp.concatenate(gather(w_3, "z"))

    both = jnp.concatenate([a_u, a_v], 1)
    pieces = [both[(4 - k) % 4 * mine :][:mine] for k in range(4)]
    got = [pieces[0]] + [shift_x(pieces[k].astype(BF), k).astype(F32) for k in (1, 2, 3)]
    same = got[0] + got[2]
    other = got[1] + got[3]
    layer0 = jnp.where(first, same, other)
    layer1 = jnp.where(first, other, same)
    up0, pre0 = layer0[:, :hidden], layer0[:, hidden:]
    pre1, up1 = layer1[:, :hidden], layer1[:, hidden:]
    side = hidden // 2
    act0 = silu_bf(pre0)
    low, high = act0[:, :side], act0[:, side:]
    near, far = jnp.where(c == 0, low, high), jnp.where(c == 0, high, low)
    pre1 = pre1 + dot(near, m_near) + dot(far, m_far)
    act1 = silu_bf(pre1)
    slope1 = slope_bf(up1, pre1)
    near, far = dot_t1(slope1, m_near), dot_t1(slope1, m_far)
    low, high = jnp.where(c == 0, near, far), jnp.where(c == 0, far, near)
    slope0 = slope_bf(up0 + jnp.concatenate([low, high], 1), pre0)

    to_first = jnp.stack([slope0, act0, slope1])
    to_last = jnp.stack([act1, slope1, act0])
    same = jnp.where(first, to_first, to_last)
    other = jnp.where(first, to_last, to_first)
    got = [same, shift_x(other, 1), shift_x(same, 2), shift_x(other, 3)]
    rpq = jnp.concatenate(got, 1)
    r_near = gather(rpq[0], "z")
    pq_near = gather(rpq[1:], "y")
    r_far = [shift(a, "c", 1) for a in r_near]
    pq_far = [shift(a, "c", 1) for a in pq_near]

    g_v = sum_back(gradient(grad_v_kernel, vs, r_near, r_far, ()), "y")
    g_u = sum_back(gradient(grad_u_kernel, us, pq_near, pq_far, (w_3,)), "z")

    squares = jnp.sum(g_u * g_u) + jnp.sum(g_v * g_v)
    for axes, count in ((("z", "y"), 16), (("p", "h", "c"), 8)):
        row = jnp.broadcast_to(squares, (count, 8, 128))
        squares = a2a(row, axes)[:, 0, 0].sum()
    grad_norm = jnp.sqrt(squares)
    factor = jnp.minimum(1.0, CLIP_NORM / grad_norm)
    g_in = jnp.where(first, g_v, g_u) * factor
    g_out = jnp.where(first, g_u, g_v) * factor
    return (g_in[None], g_out.T[None], grad_norm)


def solution(mesh):
    split = Mesh(mesh.devices.reshape(mesh.shape["pipe"], 2, 2, 4, 4), AXES)
    tensor, dp, all_model = ("h", "c"), ("z", "y"), ("h", "c", "z", "y")
    placed = (
        P(None, dp, tensor),
        P("p", all_model, None),
        P("p", None, all_model),
        P(None, dp, tensor),
    )
    return jax.shard_map(
        on_device,
        mesh=split,
        in_specs=placed,
        out_specs=(P("p", all_model, None), P("p", None, all_model), P()),
        check_vma=False,
    )
```

profile of v0, /device:TPU:0, one launch (start us, length us, event | category | flops | bytes accessed | tf_op | source)
XLA Modules:
  0.0 299.0 jit_solution(3678835976669488364)
XLA Ops:
  8.4 1.9 bitcast_select_fusion
  12.6 4.1 %cut_z.1 = (bf16[256,1024]{1,0:T(8,128)(2,1)}, bf16[256,1024]{1,0:T(8,128)(2,1)}, bf16[256,1024]{1,0:T(8,128)(2,1)}, bf16[256,1024]{1,0:T(8,128)(2,1)}) custom-call(s32[5]{0:T(128)} %stack.43.at_ref, bf16[256,4096]{1,0:T(8,128)(2,1)} %bitcast.45, bf16[256,4096]{1,0:T(8,128)(2,1)} %bitcast.43), custom_call_target="tpu_custom_call" | custom-call | tf_op jit(solution)/shard_map/cut_z/pallas_call | solution.py:81
  16.7 1.9 collective-permute-start.1
  18.6 3.6 %collective-permute-start.2 = (bf16[256,1024]{1,0:T(8,128)(2,1)}, bf16[256,1024]{1,0:T(8,128)(2,1)S(1)}, u32[]{:S(2)}, u32[]{:S(2)}) collective-permute-start(bf16[256,1024]{1,0:T(8,128)(2,1)} %get-tuple-element.35), channel_id=1, source_target_pairs={{0,8},{4,12},{8,0},{12,4},{1,9},{5,13},{9,1},{13,5},{2,10},{6,14},... | collective-permute-start | bytes 1572872 | tf_op jit(solution)/shard_map/ppermute | solution.py:36
  23.8 2.9 collective-permute-start.15
  26.7 4.1 %cut_y.1 = (bf16[256,1024]{1,0:T(8,128)(2,1)}, bf16[256,1024]{1,0:T(8,128)(2,1)}, bf16[256,1024]{1,0:T(8,128)(2,1)}, bf16[256,1024]{1,0:T(8,128)(2,1)}) custom-call(s32[5]{0:T(128)} %stack.43.at_ref, bf16[256,4096]{1,0:T(8,128)(2,1)} %bitcast.44, bf16[256,4096]{1,0:T(8,128)(2,1)} %bitcast.46), custom_call_target="tpu_custom_call" | custom-call | tf_op jit(solution)/shard_map/cut_y/pallas_call | solution.py:81
  32.8 3.0 %collective-permute-start.16 = (bf16[256,1024]{1,0:T(8,128)(2,1)}, bf16[256,1024]{1,0:T(8,128)(2,1)}, u32[]{:S(2)}, u32[]{:S(2)}) collective-permute-start(bf16[256,1024]{1,0:T(8,128)(2,1)} %get-tuple-element.86.refs_4_), channel_id=1, source_target_pairs={{0,3},{1,0},{2,1},{3,2},{4,7},{5,4},{6,5},{7,6},{8,11},{9,8},{10,9... | collective-permute-start | bytes 1572872 | tf_op jit(solution)/shard_map/ppermute | solution.py:36
  35.8 9.2 %collective-permute-done.2.refs_2_ = bf16[256,1024]{1,0:T(8,128)(2,1)S(1)} collective-permute-done((bf16[256,1024]{1,0:T(8,128)(2,1)}, bf16[256,1024]{1,0:T(8,128)(2,1)S(1)}, u32[]{:S(2)}, u32[]{:S(2)}) %collective-permute-start.2) | collective-permute-done | bytes 524320 | tf_op jit(solution)/shard_map/ppermute | solution.py:36
  47.8 9.0 %all-to-all-start = ((bf16[64,8,1024]{2,1,0:T(8,128)(2,1)}), bf16[64,8,1024]{2,1,0:T(8,128)(2,1)S(1)}, u32[]{:S(2)}, u32[]{:S(2)}) async-start(bf16[64,8,1024]{2,1,0:T(8,128)(2,1)} %bitcast.13), calls=%async_computation | async-start | bytes 2097152 | tf_op jit(solution)/shard_map/all_to_all | solution.py:31
  57.6 3.1 %collective-permute-start.5 = (bf16[256,1024]{1,0:T(8,128)(2,1)}, bf16[256,1024]{1,0:T(8,128)(2,1)S(1)}, u32[]{:S(2)}, u32[]{:S(2)}) collective-permute-start(bf16[256,1024]{1,0:T(8,128)(2,1)} %get-tuple-element.39), channel_id=1, source_target_pairs={{0,2},{1,3},{2,0},{3,1},{4,6},{5,7},{6,4},{7,5},{8,10},{9,11},{10,... | collective-permute-start | bytes 1572872 | tf_op jit(solution)/shard_map/ppermute | solution.py:36
  62.2 2.9 collective-permute-start.8
  67.6 6.3 %shard_map.68 = (bf16[512,1024]{1,0:T(8,128)(2,1)}, f32[512,1024]{1,0:T(8,128)}) custom-call(bf16[256,1024]{1,0:T(8,128)(2,1)} %get-tuple-element.33.refs_0_, bf16[256,1024]{1,0:T(8,128)(2,1)} %copy-done.17, bf16[256,1024]{1,0:T(8,128)(2,1)} %copy-done.18, bf16[256,1024]{1,0:T(8,128)(2,1)} %copy-done.19, bf16[256,1024]{1,0:T(8,128)(2,1)} %get-tuple-element.86.refs_4_, ...), custom_call_target="tpu_custom_call" | custom-call | flops 2147483648 | bytes 4194304 | tf_op jit(solution)/shard_map/pallas_call | solution.py:106
  73.9 9.2 %collective-permute-done.5.refs_2_ = bf16[256,1024]{1,0:T(8,128)(2,1)S(1)} collective-permute-done((bf16[256,1024]{1,0:T(8,128)(2,1)}, bf16[256,1024]{1,0:T(8,128)(2,1)S(1)}, u32[]{:S(2)}, u32[]{:S(2)}) %collective-permute-start.5) | collective-permute-done | bytes 524320 | tf_op jit(solution)/shard_map/ppermute | solution.py:36
  84.1 9.6 %all_to_all.21 = bf16[4,8,1024]{2,1,0:T(8,128)(2,1)} all-to-all(bf16[4,8,1024]{2,1,0:T(8,128)(2,1)S(1)} %broadcast_in_dim.18), channel_id=1, replica_groups=mesh['p'=2,'h'=2,'c'=2,'z'=4,'y'=4] {'p','h'}, dimensions={0} | all-to-all | bytes 131072 | tf_op jit(solution)/shard_map/all_to_all | solution.py:31
  95.6 6.3 %shard_map.67 = (bf16[512,1024]{1,0:T(8,128)(2,1)}, f32[512,1024]{1,0:T(8,128)}) custom-call(bf16[256,1024]{1,0:T(8,128)(2,1)} %get-tuple-element.37.refs_0_, bf16[256,1024]{1,0:T(8,128)(2,1)} %copy-done.6, bf16[256,1024]{1,0:T(8,128)(2,1)} %copy-done.7, bf16[256,1024]{1,0:T(8,128)(2,1)} %collective-permute-done.6.refs_3_, bf16[256,1024]{1,0:T(8,128)(2,1)} %copy-done, ...), custom_call_target="tpu_custom_call" | custom-call | flops 2147483648 | bytes 4194304 | tf_op jit(solution)/shard_map/pallas_call | solution.py:106
  102.9 2.3 fusion.30
  108.8 2.3 fusion.31
  116.0 2.1 collective-permute-done.19
  118.1 4.8 %collective-permute-done.20 = bf16[128,1024]{1,0:T(8,128)(2,1)S(1)} collective-permute-done((bf16[128,1024]{1,0:T(8,128)(2,1)}, bf16[128,1024]{1,0:T(8,128)(2,1)S(1)}, u32[]{:S(2)}, u32[]{:S(2)}) %collective-permute-start.20) | collective-permute-done | bytes 262176 | tf_op jit(solution)/shard_map/ppermute | solution.py:36
  123.8 4.5 %collective-permute-done.13 = bf16[128,1024]{1,0:T(8,128)(2,1)S(1)} collective-permute-done((bf16[128,1024]{1,0:T(8,128)(2,1)S(1)}, bf16[128,1024]{1,0:T(8,128)(2,1)S(1)}, u32[]{:S(2)}, u32[]{:S(2)}) %collective-permute-start.13) | collective-permute-done | bytes 262176 | tf_op jit(solution)/shard_map/ppermute | solution.py:36
  128.6 3.0 %collective-permute-start.21 = (bf16[32,2048]{1,0:T(8,128)(2,1)S(1)}, bf16[32,2048]{1,0:T(8,128)(2,1)S(1)}, u32[]{:S(2)}, u32[]{:S(2)}) collective-permute-start(bf16[32,2048]{1,0:T(8,128)(2,1)S(1)} %get-tuple-element.91), channel_id=1, source_target_pairs={{0,32},{32,0},{64,96},{96,64},{1,33},{33,1},{65,97},{97,65},{2,34}... | collective-permute-start | bytes 393224 | tf_op jit(solution)/shard_map/ppermute | solution.py:45
  131.8 3.0 %collective-permute-start.23 = (bf16[32,2048]{1,0:T(8,128)(2,1)S(1)}, bf16[32,2048]{1,0:T(8,128)(2,1)S(1)}, u32[]{:S(2)}, u32[]{:S(2)}) collective-permute-start(bf16[32,2048]{1,0:T(8,128)(2,1)S(1)} %get-tuple-element.92), channel_id=1, source_target_pairs={{0,96},{32,64},{64,0},{96,32},{1,97},{33,65},{65,1},{97,33},{2,98}... | collective-permute-start | bytes 393224 | tf_op jit(solution)/shard_map/ppermute | solution.py:45
  136.2 19.7 %all-gather.2.cloned.1.call-done = bf16[512,1024]{1,0:T(8,128)(2,1)} async-done(((bf16[32,1024]{1,0:T(8,128)(2,1)}), bf16[512,1024]{1,0:T(8,128)(2,1)}) %all-gather.2.cloned.1.call-update) | async-done | bytes 1048592 | tf_op jit(solution)/shard_map/all_gather | solution.py:224
  160.7 2.7 collective-permute-start.26
  164.8 2.3 collective-permute-start.46
  167.1 2.0 collective-permute-done.25
  169.1 3.4 %collective-permute-done.26 = bf16[3,32,1024]{2,1,0:T(8,128)(2,1)S(1)} collective-permute-done((bf16[3,32,1024]{2,1,0:T(8,128)(2,1)S(1)}, bf16[3,32,1024]{2,1,0:T(8,128)(2,1)S(1)}, u32[]{:S(2)}, u32[]{:S(2)}) %collective-permute-start.26) | collective-permute-done | bytes 196640 | tf_op jit(solution)/shard_map/ppermute | solution.py:45
  173.9 2.7 collective-permute-start.29
  177.5 2.2 collective-permute-start.39
  181.2 2.4 collective-permute-start.40
  183.6 3.1 %collective-permute-done.28.refs_5_ = bf16[128,1024]{1,0:T(8,128)(2,1)S(1)} collective-permute-done((bf16[128,1024]{1,0:T(8,128)(2,1)S(1)}, bf16[128,1024]{1,0:T(8,128)(2,1)S(1)}, u32[]{:S(2)}, u32[]{:S(2)}) %collective-permute-start.28) | collective-permute-done | bytes 262176 | tf_op jit(solution)/shard_map/ppermute | solution.py:36
  187.3 3.4 %collective-permute-done.29.refs_6_ = bf16[128,1024]{1,0:T(8,128)(2,1)S(1)} collective-permute-done((bf16[128,1024]{1,0:T(8,128)(2,1)S(1)}, bf16[128,1024]{1,0:T(8,128)(2,1)S(1)}, u32[]{:S(2)}, u32[]{:S(2)}) %collective-permute-start.29) | collective-permute-done | bytes 262176 | tf_op jit(solution)/shard_map/ppermute | solution.py:36
  190.7 4.1 %collective-permute-done.30.refs_7_ = bf16[128,1024]{1,0:T(8,128)(2,1)S(1)} collective-permute-done((bf16[128,1024]{1,0:T(8,128)(2,1)S(1)}, bf16[128,1024]{1,0:T(8,128)(2,1)S(1)}, u32[]{:S(2)}, u32[]{:S(2)}) %collective-permute-start.30) | collective-permute-done | bytes 262176 | tf_op jit(solution)/shard_map/ppermute | solution.py:36
  196.4 5.2 %collective-permute-done.38.refs_5_ = bf16[2,128,1024]{2,1,0:T(8,128)(2,1)S(1)} collective-permute-done((bf16[2,128,1024]{2,1,0:T(8,128)(2,1)S(1)}, bf16[2,128,1024]{2,1,0:T(8,128)(2,1)S(1)}, u32[]{:S(2)}, u32[]{:S(2)}) %collective-permute-start.38) | collective-permute-done | bytes 524320 | tf_op jit(solution)/shard_map/ppermute | solution.py:36
  204.7 6.8 %shard_map.69 = (f32[256,1024]{1,0:T(8,128)}, bf16[256,1024]{1,0:T(8,128)(2,1)}, bf16[256,1024]{1,0:T(8,128)(2,1)}, bf16[256,1024]{1,0:T(8,128)(2,1)}) custom-call(bf16[256,1024]{1,0:T(8,128)(2,1)} %get-tuple-element.33.refs_0_, bf16[256,1024]{1,0:T(8,128)(2,1)} %copy-done.17, bf16[256,1024]{1,0:T(8,128)(2,1)} %copy-done.18, bf16[256,1024]{1,0:T(8,128)(2,1)} %copy-done.19, ...), custom_call_target="tpu_custom_call" | custom-call | flops 2147483648 | bytes 4194304 | tf_op jit(solution)/shard_map/pallas_call | solution.py:165
  211.6 2.4 collective-permute-start.35
  215.4 2.8 pad_maximum_fusion.refs_12_
  218.2 13.0 %shard_map.70 = (f32[256,1024]{1,0:T(8,128)}, bf16[256,1024]{1,0:T(8,128)(2,1)}, bf16[256,1024]{1,0:T(8,128)(2,1)}, bf16[256,1024]{1,0:T(8,128)(2,1)}) custom-call(bf16[256,1024]{1,0:T(8,128)(2,1)} %get-tuple-element.37.refs_0_, bf16[256,1024]{1,0:T(8,128)(2,1)} %copy-done.6, bf16[256,1024]{1,0:T(8,128)(2,1)} %copy-done.7, ...), custom_call_target="tpu_custom_call" | custom-call | flops 2147483648 | bytes 4194304 | tf_op jit(solution)/shard_map/pallas_call | solution.py:165
  234.3 3.1 %collective-permute-done.35 = bf16[256,1024]{1,0:T(8,128)(2,1)} collective-permute-done((bf16[256,1024]{1,0:T(8,128)(2,1)}, bf16[256,1024]{1,0:T(8,128)(2,1)}, u32[]{:S(2)}, u32[]{:S(2)}) %collective-permute-start.35) | collective-permute-done | bytes 524320 | tf_op jit(solution)/shard_map/ppermute | solution.py:36
  237.9 3.0 %collective-permute-done.37 = bf16[256,1024]{1,0:T(8,128)(2,1)S(1)} collective-permute-done((bf16[256,1024]{1,0:T(8,128)(2,1)}, bf16[256,1024]{1,0:T(8,128)(2,1)S(1)}, u32[]{:S(2)}, u32[]{:S(2)}) %collective-permute-start.37) | collective-permute-done | bytes 524320 | tf_op jit(solution)/shard_map/ppermute | solution.py:36
  241.7 2.3 multiply_reduce_fusion
  244.0 2.3 collective-permute-done.48
  246.3 2.9 collective-permute-done.49
  249.2 9.9 %collective-permute-done.50 = bf16[256,1024]{1,0:T(8,128)(2,1)S(1)} collective-permute-done((bf16[256,1024]{1,0:T(8,128)(2,1)}, bf16[256,1024]{1,0:T(8,128)(2,1)S(1)}, u32[]{:S(2)}, u32[]{:S(2)}) %collective-permute-start.50) | collective-permute-done | bytes 524320 | tf_op jit(solution)/shard_map/ppermute | solution.py:36
  259.1 1.9 multiply_reduce_fusion.1
  262.3 12.4 %all_to_all.22 = f32[16,8,128]{2,1,0:T(8,128)S(1)} all-to-all(f32[16,8,128]{2,1,0:T(8,128)S(1)} %broadcast_in_dim.19), channel_id=1, replica_groups=mesh['p'=2,'h'=2,'c'=2,'z'=4,'y'=4] {'z','y'}, dimensions={0} | all-to-all | bytes 131072 | tf_op jit(solution)/shard_map/all_to_all | solution.py:31
  276.0 9.9 %all_to_all.23 = f32[8,8,128]{2,1,0:T(8,128)S(1)} all-to-all(f32[8,8,128]{2,1,0:T(8,128)S(1)} %broadcast_in_dim.20), channel_id=1, replica_groups=mesh['p'=2,'h'=2,'c'=2,'z'=4,'y'=4] {'p','h','c'}, dimensions={0} | all-to-all | bytes 65536 | tf_op jit(solution)/shard_map/all_to_all | solution.py:31
  287.2 2.5 multiply_bitcast_fusion
  (160 shorter events, 54.1 us)
Async XLA Ops:
  10.4 20.4 %collective-permute-start = (bf16[256,1024]{1,0:T(8,128)(2,1)S(1)}, bf16[256,1024]{1,0:T(8,128)(2,1)S(1)}, u32[]{:S(2)}, u32[]{:S(2)}) collective-permute-start(bf16[256,1024]{1,0:T(8,128)(2,1)S(1)} %get-tuple-element.42.refs_4_), channel_id=1, source_target_pairs={{0,64},{64,0},{1,65},{65,1},{2,66},{66,2},{3,67},{67,3},{4,68},{68... | collective-permute-start | bytes 1572872 | tf_op jit(solution)/shard_map/ppermute | solution.py:205
  16.7 16.1 %collective-permute-start.1 = (bf16[256,1024]{1,0:T(8,128)(2,1)}, bf16[256,1024]{1,0:T(8,128)(2,1)S(1)}, u32[]{:S(2)}, u32[]{:S(2)}) collective-permute-start(bf16[256,1024]{1,0:T(8,128)(2,1)} %get-tuple-element.34), channel_id=1, source_target_pairs={{0,4},{4,8},{8,12},{12,0},{1,5},{5,9},{9,13},{13,1},{2,6},{6,10},{... | collective-permute-start | bytes 1572872 | tf_op jit(solution)/shard_map/ppermute | solution.py:36
  18.6 26.4 %collective-permute-start.2 = (bf16[256,1024]{1,0:T(8,128)(2,1)}, bf16[256,1024]{1,0:T(8,128)(2,1)S(1)}, u32[]{:S(2)}, u32[]{:S(2)}) collective-permute-start(bf16[256,1024]{1,0:T(8,128)(2,1)} %get-tuple-element.35), channel_id=1, source_target_pairs={{0,8},{4,12},{8,0},{12,4},{1,9},{5,13},{9,1},{13,5},{2,10},{6,14},... | collective-permute-start | bytes 1572872 | tf_op jit(solution)/shard_map/ppermute | solution.py:36
  22.2 38.5 %collective-permute-start.14 = (bf16[256,1024]{1,0:T(8,128)(2,1)}, bf16[256,1024]{1,0:T(8,128)(2,1)}, u32[]{:S(2)}, u32[]{:S(2)}) collective-permute-start(bf16[256,1024]{1,0:T(8,128)(2,1)} %get-tuple-element.86.refs_4_), channel_id=1, source_target_pairs={{0,1},{1,2},{2,3},{3,0},{4,5},{5,6},{6,7},{7,4},{8,9},{9,10},{10,1... | collective-permute-start | bytes 1572872 | tf_op jit(solution)/shard_map/ppermute | solution.py:36
  23.8 38.4 %collective-permute-start.15 = (bf16[256,1024]{1,0:T(8,128)(2,1)}, bf16[256,1024]{1,0:T(8,128)(2,1)}, u32[]{:S(2)}, u32[]{:S(2)}) collective-permute-start(bf16[256,1024]{1,0:T(8,128)(2,1)} %get-tuple-element.86.refs_4_), channel_id=1, source_target_pairs={{0,2},{1,3},{2,0},{3,1},{4,6},{5,7},{6,4},{7,5},{8,10},{9,11},{10,... | collective-permute-start | bytes 1572872 | tf_op jit(solution)/shard_map/ppermute | solution.py:36
  30.8 26.0 %collective-permute-start.3 = (bf16[256,1024]{1,0:T(8,128)(2,1)}, bf16[256,1024]{1,0:T(8,128)(2,1)S(1)}, u32[]{:S(2)}, u32[]{:S(2)}) collective-permute-start(bf16[256,1024]{1,0:T(8,128)(2,1)} %get-tuple-element.36), channel_id=1, source_target_pairs={{0,12},{4,0},{8,4},{12,8},{1,13},{5,1},{9,5},{13,9},{2,14},{6,2},{... | collective-permute-start | bytes 1572872 | tf_op jit(solution)/shard_map/ppermute | solution.py:36
  32.8 32.3 %collective-permute-start.16 = (bf16[256,1024]{1,0:T(8,128)(2,1)}, bf16[256,1024]{1,0:T(8,128)(2,1)}, u32[]{:S(2)}, u32[]{:S(2)}) collective-permute-start(bf16[256,1024]{1,0:T(8,128)(2,1)} %get-tuple-element.86.refs_4_), channel_id=1, source_target_pairs={{0,3},{1,0},{2,1},{3,2},{4,7},{5,4},{6,5},{7,6},{8,11},{9,8},{10,9... | collective-permute-start | bytes 1572872 | tf_op jit(solution)/shard_map/ppermute | solution.py:36
  45.0 21.5 %collective-permute-start.4 = (bf16[256,1024]{1,0:T(8,128)(2,1)}, bf16[256,1024]{1,0:T(8,128)(2,1)S(1)}, u32[]{:S(2)}, u32[]{:S(2)}) collective-permute-start(bf16[256,1024]{1,0:T(8,128)(2,1)} %get-tuple-element.38), channel_id=1, source_target_pairs={{0,1},{1,2},{2,3},{3,0},{4,5},{5,6},{6,7},{7,4},{8,9},{9,10},{10,1... | collective-permute-start | bytes 1572872 | tf_op jit(solution)/shard_map/ppermute | solution.py:36
  47.8 36.2 %all-to-all-start = ((bf16[64,8,1024]{2,1,0:T(8,128)(2,1)}), bf16[64,8,1024]{2,1,0:T(8,128)(2,1)S(1)}, u32[]{:S(2)}, u32[]{:S(2)}) async-start(bf16[64,8,1024]{2,1,0:T(8,128)(2,1)} %bitcast.13), calls=%async_computation | async-start | bytes 2097152 | tf_op jit(solution)/shard_map/all_to_all | solution.py:31
  56.7 99.1 %all-gather.2.cloned.1.call-start = ((), (), s32[]{:S(2)}) async-start(), calls=%async_computation.4 | async-start | bytes 1114112 | tf_op jit(solution)/shard_map/all_gather | solution.py:224
  57.6 25.5 %collective-permute-start.5 = (bf16[256,1024]{1,0:T(8,128)(2,1)}, bf16[256,1024]{1,0:T(8,128)(2,1)S(1)}, u32[]{:S(2)}, u32[]{:S(2)}) collective-permute-start(bf16[256,1024]{1,0:T(8,128)(2,1)} %get-tuple-element.39), channel_id=1, source_target_pairs={{0,2},{1,3},{2,0},{3,1},{4,6},{5,7},{6,4},{7,5},{8,10},{9,11},{10,... | collective-permute-start | bytes 1572872 | tf_op jit(solution)/shard_map/ppermute | solution.py:36
  60.7 33.0 %collective-permute-start.7 = (bf16[256,1024]{1,0:T(8,128)(2,1)S(1)}, bf16[256,1024]{1,0:T(8,128)(2,1)}, u32[]{:S(2)}, u32[]{:S(2)}) collective-permute-start(bf16[256,1024]{1,0:T(8,128)(2,1)S(1)} %get-tuple-element.42.refs_4_), channel_id=1, source_target_pairs={{0,4},{4,8},{8,12},{12,0},{1,5},{5,9},{9,13},{13,1},{2,6},{6,10},{... | collective-permute-start | bytes 1572872 | tf_op jit(solution)/shard_map/ppermute | solution.py:36
  62.2 33.4 %collective-permute-start.8 = (bf16[256,1024]{1,0:T(8,128)(2,1)S(1)}, bf16[256,1024]{1,0:T(8,128)(2,1)}, u32[]{:S(2)}, u32[]{:S(2)}) collective-permute-start(bf16[256,1024]{1,0:T(8,128)(2,1)S(1)} %get-tuple-element.42.refs_4_), channel_id=1, source_target_pairs={{0,8},{4,12},{8,0},{12,4},{1,9},{5,13},{9,1},{13,5},{2,10},{6,14},... | collective-permute-start | bytes 1572872 | tf_op jit(solution)/shard_map/ppermute | solution.py:36
  65.1 30.5 %collective-permute-start.9 = (bf16[256,1024]{1,0:T(8,128)(2,1)S(1)}, bf16[256,1024]{1,0:T(8,128)(2,1)}, u32[]{:S(2)}, u32[]{:S(2)}) collective-permute-start(bf16[256,1024]{1,0:T(8,128)(2,1)S(1)} %get-tuple-element.42.refs_4_), channel_id=1, source_target_pairs={{0,12},{4,0},{8,4},{12,8},{1,13},{5,1},{9,5},{13,9},{2,14},{6,2},{... | collective-permute-start | bytes 1572872 | tf_op jit(solution)/shard_map/ppermute | solution.py:36
  66.5 27.3 %collective-permute-start.6 = (bf16[256,1024]{1,0:T(8,128)(2,1)}, bf16[256,1024]{1,0:T(8,128)(2,1)}, u32[]{:S(2)}, u32[]{:S(2)}) collective-permute-start(bf16[256,1024]{1,0:T(8,128)(2,1)} %get-tuple-element.40), channel_id=1, source_target_pairs={{0,3},{1,0},{2,1},{3,2},{4,7},{5,4},{6,5},{7,6},{8,11},{9,8},{10,9... | collective-permute-start | bytes 1572872 | tf_op jit(solution)/shard_map/ppermute | solution.py:36
  83.9 18.0 %collective-permute-start.17 = (bf16[512,1024]{1,0:T(8,128)(2,1)}, bf16[512,1024]{1,0:T(8,128)(2,1)S(1)}, u32[]{:S(2)}, u32[]{:S(2)}) collective-permute-start(bf16[512,1024]{1,0:T(8,128)(2,1)} %get-tuple-element.46), channel_id=1, source_target_pairs={{0,16},{16,0},{1,17},{17,1},{2,18},{18,2},{3,19},{19,3},{4,20},{20... | collective-permute-start | bytes 3145736 | tf_op jit(solution)/shard_map/ppermute | solution.py:36
  106.0 9.4 %collective-permute-start.18 = (bf16[128,1024]{1,0:T(8,128)(2,1)}, bf16[128,1024]{1,0:T(8,128)(2,1)S(1)}, u32[]{:S(2)}, u32[]{:S(2)}) collective-permute-start(bf16[128,1024]{1,0:T(8,128)(2,1)} %get-tuple-element.83), channel_id=1, source_target_pairs={{0,12},{4,0},{8,4},{12,8},{1,13},{5,1},{9,5},{13,9},{2,14},{6,2},{... | collective-permute-start | bytes 786440 | tf_op jit(solution)/shard_map/ppermute | solution.py:36
  107.2 10.9 %collective-permute-start.19 = (bf16[128,1024]{1,0:T(8,128)(2,1)}, bf16[128,1024]{1,0:T(8,128)(2,1)S(1)}, u32[]{:S(2)}, u32[]{:S(2)}) collective-permute-start(bf16[128,1024]{1,0:T(8,128)(2,1)} %get-tuple-element.85), channel_id=1, source_target_pairs={{0,8},{4,12},{8,0},{12,4},{1,9},{5,13},{9,1},{13,5},{2,10},{6,14},... | collective-permute-start | bytes 786440 | tf_op jit(solution)/shard_map/ppermute | solution.py:36
  108.4 14.5 %collective-permute-start.20 = (bf16[128,1024]{1,0:T(8,128)(2,1)}, bf16[128,1024]{1,0:T(8,128)(2,1)S(1)}, u32[]{:S(2)}, u32[]{:S(2)}) collective-permute-start(bf16[128,1024]{1,0:T(8,128)(2,1)} %get-tuple-element.84), channel_id=1, source_target_pairs={{0,4},{4,8},{8,12},{12,0},{1,5},{5,9},{9,13},{13,1},{2,6},{6,10},{... | collective-permute-start | bytes 786440 | tf_op jit(solution)/shard_map/ppermute | solution.py:36
  111.2 11.9 %collective-permute-start.11 = (bf16[128,1024]{1,0:T(8,128)(2,1)S(1)}, bf16[128,1024]{1,0:T(8,128)(2,1)S(1)}, u32[]{:S(2)}, u32[]{:S(2)}) collective-permute-start(bf16[128,1024]{1,0:T(8,128)(2,1)S(1)} %get-tuple-element.88), channel_id=1, source_target_pairs={{0,3},{1,0},{2,1},{3,2},{4,7},{5,4},{6,5},{7,6},{8,11},{9,8},{10,9... | collective-permute-start | bytes 786440 | tf_op jit(solution)/shard_map/ppermute | solution.py:36
  113.0 10.8 %collective-permute-start.12 = (bf16[128,1024]{1,0:T(8,128)(2,1)S(1)}, bf16[128,1024]{1,0:T(8,128)(2,1)S(1)}, u32[]{:S(2)}, u32[]{:S(2)}) collective-permute-start(bf16[128,1024]{1,0:T(8,128)(2,1)S(1)} %get-tuple-element.90), channel_id=1, source_target_pairs={{0,2},{1,3},{2,0},{3,1},{4,6},{5,7},{6,4},{7,5},{8,10},{9,11},{10,... | collective-permute-start | bytes 786440 | tf_op jit(solution)/shard_map/ppermute | solution.py:36
  115.4 12.8 %collective-permute-start.13 = (bf16[128,1024]{1,0:T(8,128)(2,1)S(1)}, bf16[128,1024]{1,0:T(8,128)(2,1)S(1)}, u32[]{:S(2)}, u32[]{:S(2)}) collective-permute-start(bf16[128,1024]{1,0:T(8,128)(2,1)S(1)} %get-tuple-element.89), channel_id=1, source_target_pairs={{0,1},{1,2},{2,3},{3,0},{4,5},{5,6},{6,7},{7,4},{8,9},{9,10},{10,1... | collective-permute-start | bytes 786440 | tf_op jit(solution)/shard_map/ppermute | solution.py:36
  128.6 27.3 %collective-permute-start.21 = (bf16[32,2048]{1,0:T(8,128)(2,1)S(1)}, bf16[32,2048]{1,0:T(8,128)(2,1)S(1)}, u32[]{:S(2)}, u32[]{:S(2)}) collective-permute-start(bf16[32,2048]{1,0:T(8,128)(2,1)S(1)} %get-tuple-element.91), channel_id=1, source_target_pairs={{0,32},{32,0},{64,96},{96,64},{1,33},{33,1},{65,97},{97,65},{2,34}... | collective-permute-start | bytes 393224 | tf_op jit(solution)/shard_map/ppermute | solution.py:45
  131.6 24.3 %collective-permute-start.22 = (bf16[32,2048]{1,0:T(8,128)(2,1)S(1)}, bf16[32,2048]{1,0:T(8,128)(2,1)S(1)}, u32[]{:S(2)}, u32[]{:S(2)}) collective-permute-start(bf16[32,2048]{1,0:T(8,128)(2,1)S(1)} %get-tuple-element.93), channel_id=1, source_target_pairs={{0,64},{32,96},{64,32},{96,0},{1,65},{33,97},{65,33},{97,1},{2,66}... | collective-permute-start | bytes 393224 | tf_op jit(solution)/shard_map/ppermute | solution.py:45
  131.8 24.0 %collective-permute-start.23 = (bf16[32,2048]{1,0:T(8,128)(2,1)S(1)}, bf16[32,2048]{1,0:T(8,128)(2,1)S(1)}, u32[]{:S(2)}, u32[]{:S(2)}) collective-permute-start(bf16[32,2048]{1,0:T(8,128)(2,1)S(1)} %get-tuple-element.92), channel_id=1, source_target_pairs={{0,96},{32,64},{64,0},{96,32},{1,97},{33,65},{65,1},{97,33},{2,98}... | collective-permute-start | bytes 393224 | tf_op jit(solution)/shard_map/ppermute | solution.py:45
  134.9 42.6 %collective-permute-start.45 = (bf16[256,1024]{1,0:T(8,128)(2,1)S(1)}, bf16[256,1024]{1,0:T(8,128)(2,1)S(1)}, u32[]{:S(2)}, u32[]{:S(2)}) collective-permute-start(bf16[256,1024]{1,0:T(8,128)(2,1)S(1)} %collective-permute-done), channel_id=1, source_target_pairs={{0,4},{4,8},{8,12},{12,0},{1,5},{5,9},{9,13},{13,1},{2,6},{6,10},{... | collective-permute-start | bytes 1572872 | tf_op jit(solution)/shard_map/ppermute | solution.py:36
  160.1 9.1 %collective-permute-start.25 = (bf16[3,32,1024]{2,1,0:T(8,128)(2,1)S(1)}, bf16[3,32,1024]{2,1,0:T(8,128)(2,1)S(1)}, u32[]{:S(2)}, u32[]{:S(2)}) collective-permute-start(bf16[3,32,1024]{2,1,0:T(8,128)(2,1)S(1)} %get-tuple-element.95), channel_id=1, source_target_pairs={{0,64},{32,96},{64,32},{96,0},{1,65},{33,97},{65,33},{97,1},{2,66}... | collective-permute-start | bytes 589832 | tf_op jit(solution)/shard_map/ppermute | solution.py:45
  160.7 11.8 %collective-permute-start.26 = (bf16[3,32,1024]{2,1,0:T(8,128)(2,1)S(1)}, bf16[3,32,1024]{2,1,0:T(8,128)(2,1)S(1)}, u32[]{:S(2)}, u32[]{:S(2)}) collective-permute-start(bf16[3,32,1024]{2,1,0:T(8,128)(2,1)S(1)} %get-tuple-element.94), channel_id=1, source_target_pairs={{0,32},{32,0},{64,96},{96,64},{1,33},{33,1},{65,97},{97,65},{2,34}... | collective-permute-start | bytes 589832 | tf_op jit(solution)/shard_map/ppermute | solution.py:45
  163.4 9.8 %collective-permute-start.27 = (bf16[3,32,1024]{2,1,0:T(8,128)(2,1)S(1)}, bf16[3,32,1024]{2,1,0:T(8,128)(2,1)S(1)}, u32[]{:S(2)}, u32[]{:S(2)}) collective-permute-start(bf16[3,32,1024]{2,1,0:T(8,128)(2,1)S(1)} %get-tuple-element.95), channel_id=1, source_target_pairs={{0,96},{32,64},{64,0},{96,32},{1,97},{33,65},{65,1},{97,33},{2,98}... | collective-permute-start | bytes 589832 | tf_op jit(solution)/shard_map/ppermute | solution.py:45
  164.8 16.3 %collective-permute-start.46 = (bf16[256,1024]{1,0:T(8,128)(2,1)S(1)}, bf16[256,1024]{1,0:T(8,128)(2,1)S(1)}, u32[]{:S(2)}, u32[]{:S(2)}) collective-permute-start(bf16[256,1024]{1,0:T(8,128)(2,1)S(1)} %collective-permute-done), channel_id=1, source_target_pairs={{0,8},{4,12},{8,0},{12,4},{1,9},{5,13},{9,1},{13,5},{2,10},{6,14},... | collective-permute-start | bytes 1572872 | tf_op jit(solution)/shard_map/ppermute | solution.py:36
  173.2 13.6 %collective-permute-start.28 = (bf16[128,1024]{1,0:T(8,128)(2,1)S(1)}, bf16[128,1024]{1,0:T(8,128)(2,1)S(1)}, u32[]{:S(2)}, u32[]{:S(2)}) collective-permute-start(bf16[128,1024]{1,0:T(8,128)(2,1)S(1)} %maximum_bitcast_fusion.refs_4_), channel_id=1, source_target_pairs={{0,4},{4,8},{8,12},{12,0},{1,5},{5,9},{9,13},{13,1},{2,6},{6,10},{... | collective-permute-start | bytes 786440 | tf_op jit(solution)/shard_map/ppermute | solution.py:36
  173.9 16.8 %collective-permute-start.29 = (bf16[128,1024]{1,0:T(8,128)(2,1)S(1)}, bf16[128,1024]{1,0:T(8,128)(2,1)S(1)}, u32[]{:S(2)}, u32[]{:S(2)}) collective-permute-start(bf16[128,1024]{1,0:T(8,128)(2,1)S(1)} %maximum_bitcast_fusion.refs_4_), channel_id=1, source_target_pairs={{0,8},{4,12},{8,0},{12,4},{1,9},{5,13},{9,1},{13,5},{2,10},{6,14},... | collective-permute-start | bytes 786440 | tf_op jit(solution)/shard_map/ppermute | solution.py:36
  176.6 24.9 %collective-permute-start.38 = (bf16[2,128,1024]{2,1,0:T(8,128)(2,1)S(1)}, bf16[2,128,1024]{2,1,0:T(8,128)(2,1)S(1)}, u32[]{:S(2)}, u32[]{:S(2)}) collective-permute-start(bf16[2,128,1024]{2,1,0:T(8,128)(2,1)S(1)} %pad_maximum_fusion.1.refs_4_), channel_id=1, source_target_pairs={{0,1},{1,2},{2,3},{3,0},{4,5},{5,6},{6,7},{7,4},{8,9},{9,10},{10,1... | collective-permute-start | bytes 1572872 | tf_op jit(solution)/shard_map/ppermute | solution.py:36
  177.5 24.1 %collective-permute-start.39 = (bf16[2,128,1024]{2,1,0:T(8,128)(2,1)S(1)}, bf16[2,128,1024]{2,1,0:T(8,128)(2,1)S(1)}, u32[]{:S(2)}, u32[]{:S(2)}) collective-permute-start(bf16[2,128,1024]{2,1,0:T(8,128)(2,1)S(1)} %pad_maximum_fusion.1.refs_4_), channel_id=1, source_target_pairs={{0,2},{1,3},{2,0},{3,1},{4,6},{5,7},{6,4},{7,5},{8,10},{9,11},{10,... | collective-permute-start | bytes 1572872 | tf_op jit(solution)/shard_map/ppermute | solution.py:36
  181.2 21.1 %collective-permute-start.40 = (bf16[2,128,1024]{2,1,0:T(8,128)(2,1)S(1)}, bf16[2,128,1024]{2,1,0:T(8,128)(2,1)}, u32[]{:S(2)}, u32[]{:S(2)}) collective-permute-start(bf16[2,128,1024]{2,1,0:T(8,128)(2,1)S(1)} %pad_maximum_fusion.1.refs_4_), channel_id=1, source_target_pairs={{0,3},{1,0},{2,1},{3,2},{4,7},{5,4},{6,5},{7,6},{8,11},{9,8},{10,9... | collective-permute-start | bytes 1572872 | tf_op jit(solution)/shard_map/ppermute | solution.py:36
  186.7 8.1 %collective-permute-start.30 = (bf16[128,1024]{1,0:T(8,128)(2,1)S(1)}, bf16[128,1024]{1,0:T(8,128)(2,1)S(1)}, u32[]{:S(2)}, u32[]{:S(2)}) collective-permute-start(bf16[128,1024]{1,0:T(8,128)(2,1)S(1)} %maximum_bitcast_fusion.refs_4_), channel_id=1, source_target_pairs={{0,12},{4,0},{8,4},{12,8},{1,13},{5,1},{9,5},{13,9},{2,14},{6,2},{... | collective-permute-start | bytes 786440 | tf_op jit(solution)/shard_map/ppermute | solution.py:36
  194.8 7.5 %collective-permute-start.32 = (bf16[128,1024]{1,0:T(8,128)(2,1)S(1)}, bf16[128,1024]{1,0:T(8,128)(2,1)S(1)}, u32[]{:S(2)}, u32[]{:S(2)}) collective-permute-start(bf16[128,1024]{1,0:T(8,128)(2,1)S(1)} %collective-permute-done.28.refs_5_), channel_id=1, source_target_pairs={{0,16},{16,0},{1,17},{17,1},{2,18},{18,2},{3,19},{19,3},{4,20},{20... | collective-permute-start | bytes 786440 | tf_op jit(solution)/shard_map/ppermute | solution.py:36
  194.8 16.7 %collective-permute-start.47 = (bf16[256,1024]{1,0:T(8,128)(2,1)S(1)}, bf16[256,1024]{1,0:T(8,128)(2,1)}, u32[]{:S(2)}, u32[]{:S(2)}) collective-permute-start(bf16[256,1024]{1,0:T(8,128)(2,1)S(1)} %collective-permute-done), channel_id=1, source_target_pairs={{0,12},{4,0},{8,4},{12,8},{1,13},{5,1},{9,5},{13,9},{2,14},{6,2},{... | collective-permute-start | bytes 1572872 | tf_op jit(solution)/shard_map/ppermute | solution.py:36
  202.3 11.6 %collective-permute-start.41 = (bf16[2,128,1024]{2,1,0:T(8,128)(2,1)S(1)}, bf16[2,128,1024]{2,1,0:T(8,128)(2,1)S(1)}, u32[]{:S(2)}, u32[]{:S(2)}) collective-permute-start(bf16[2,128,1024]{2,1,0:T(8,128)(2,1)S(1)} %pad_maximum_fusion.1.refs_4_), channel_id=1, source_target_pairs={{0,16},{16,0},{1,17},{17,1},{2,18},{18,2},{3,19},{19,3},{4,20},{20... | collective-permute-start | bytes 1572872 | tf_op jit(solution)/shard_map/ppermute | solution.py:36
  202.3 12.2 %collective-permute-start.42 = (bf16[2,128,1024]{2,1,0:T(8,128)(2,1)S(1)}, bf16[2,128,1024]{2,1,0:T(8,128)(2,1)S(1)}, u32[]{:S(2)}, u32[]{:S(2)}) collective-permute-start(bf16[2,128,1024]{2,1,0:T(8,128)(2,1)S(1)} %collective-permute-done.38.refs_5_), channel_id=1, source_target_pairs={{0,16},{16,0},{1,17},{17,1},{2,18},{18,2},{3,19},{19,3},{4,20},{20... | collective-permute-start | bytes 1572872 | tf_op jit(solution)/shard_map/ppermute | solution.py:36
  203.1 15.1 %collective-permute-start.43 = (bf16[2,128,1024]{2,1,0:T(8,128)(2,1)S(1)}, bf16[2,128,1024]{2,1,0:T(8,128)(2,1)}, u32[]{:S(2)}, u32[]{:S(2)}) collective-permute-start(bf16[2,128,1024]{2,1,0:T(8,128)(2,1)S(1)} %collective-permute-done.39.refs_6_), channel_id=1, source_target_pairs={{0,16},{16,0},{1,17},{17,1},{2,18},{18,2},{3,19},{19,3},{4,20},{20... | collective-permute-start | bytes 1572872 | tf_op jit(solution)/shard_map/ppermute | solution.py:36
  204.5 13.7 %collective-permute-start.44 = (bf16[2,128,1024]{2,1,0:T(8,128)(2,1)}, bf16[2,128,1024]{2,1,0:T(8,128)(2,1)}, u32[]{:S(2)}, u32[]{:S(2)}) collective-permute-start(bf16[2,128,1024]{2,1,0:T(8,128)(2,1)} %collective-permute-done.40.refs_7_), channel_id=1, source_target_pairs={{0,16},{16,0},{1,17},{17,1},{2,18},{18,2},{3,19},{19,3},{4,20},{20... | collective-permute-start | bytes 1572872 | tf_op jit(solution)/shard_map/ppermute | solution.py:36
  211.6 25.8 %collective-permute-start.35 = (bf16[256,1024]{1,0:T(8,128)(2,1)}, bf16[256,1024]{1,0:T(8,128)(2,1)}, u32[]{:S(2)}, u32[]{:S(2)}) collective-permute-start(bf16[256,1024]{1,0:T(8,128)(2,1)} %get-tuple-element.51), channel_id=1, source_target_pairs={{0,3},{1,0},{2,1},{3,2},{4,7},{5,4},{6,5},{7,6},{8,11},{9,8},{10,9... | collective-permute-start | bytes 1572872 | tf_op jit(solution)/shard_map/ppermute | solution.py:36
  214.0 24.0 %collective-permute-start.36 = (bf16[256,1024]{1,0:T(8,128)(2,1)}, bf16[256,1024]{1,0:T(8,128)(2,1)S(1)}, u32[]{:S(2)}, u32[]{:S(2)}) collective-permute-start(bf16[256,1024]{1,0:T(8,128)(2,1)} %get-tuple-element.52), channel_id=1, source_target_pairs={{0,2},{1,3},{2,0},{3,1},{4,6},{5,7},{6,4},{7,5},{8,10},{9,11},{10,... | collective-permute-start | bytes 1572872 | tf_op jit(solution)/shard_map/ppermute | solution.py:36
  214.6 26.4 %collective-permute-start.37 = (bf16[256,1024]{1,0:T(8,128)(2,1)}, bf16[256,1024]{1,0:T(8,128)(2,1)S(1)}, u32[]{:S(2)}, u32[]{:S(2)}) collective-permute-start(bf16[256,1024]{1,0:T(8,128)(2,1)} %get-tuple-element.53), channel_id=1, source_target_pairs={{0,1},{1,2},{2,3},{3,0},{4,5},{5,6},{6,7},{7,4},{8,9},{9,10},{10,1... | collective-permute-start | bytes 1572872 | tf_op jit(solution)/shard_map/ppermute | solution.py:36
  231.2 15.1 %collective-permute-start.48 = (bf16[256,1024]{1,0:T(8,128)(2,1)}, bf16[256,1024]{1,0:T(8,128)(2,1)S(1)}, u32[]{:S(2)}, u32[]{:S(2)}) collective-permute-start(bf16[256,1024]{1,0:T(8,128)(2,1)} %get-tuple-element.56), channel_id=1, source_target_pairs={{0,12},{4,0},{8,4},{12,8},{1,13},{5,1},{9,5},{13,9},{2,14},{6,2},{... | collective-permute-start | bytes 1572872 | tf_op jit(solution)/shard_map/ppermute | solution.py:36
  232.7 16.6 %collective-permute-start.49 = (bf16[256,1024]{1,0:T(8,128)(2,1)}, bf16[256,1024]{1,0:T(8,128)(2,1)S(1)}, u32[]{:S(2)}, u32[]{:S(2)}) collective-permute-start(bf16[256,1024]{1,0:T(8,128)(2,1)} %get-tuple-element.57), channel_id=1, source_target_pairs={{0,8},{4,12},{8,0},{12,4},{1,9},{5,13},{9,1},{13,5},{2,10},{6,14},... | collective-permute-start | bytes 1572872 | tf_op jit(solution)/shard_map/ppermute | solution.py:36
  237.4 21.7 %collective-permute-start.50 = (bf16[256,1024]{1,0:T(8,128)(2,1)}, bf16[256,1024]{1,0:T(8,128)(2,1)S(1)}, u32[]{:S(2)}, u32[]{:S(2)}) collective-permute-start(bf16[256,1024]{1,0:T(8,128)(2,1)} %get-tuple-element.58), channel_id=1, source_target_pairs={{0,4},{4,8},{8,12},{12,0},{1,5},{5,9},{9,13},{13,1},{2,6},{6,10},{... | collective-permute-start | bytes 1572872 | tf_op jit(solution)/shard_map/ppermute | solution.py:36
  (32 other events, 340.8 us)
Sparse Core Ops, SparseCore 0:
  108.9 46.8 all-gather.1
where the time goes:
time: 300 us; the launch traced here: 299 us
  waiting for transfers between devices  99.6 us (33%)
  starting transfers between devices  76.6 us (26%)
  Pallas kernels  40.6 us (14%)
  blocking collectives  31.9 us (11%)
  other arithmetic  18 us (6%)
  between operations  17.6 us (6%)
  local copies, waits for them, and re-layouts  11.1 us (4%)
  matrix products  3.51 us (1%)
    ppermute x44, waiting for transfers between devices, shift(): lax.ppermute(value, axis, [(i, (i + by) % count) for i in range(count)])  73.9 us
    ppermute x44, starting transfers between devices, shift(): lax.ppermute(value, axis, [(i, (i + by) % count) for i in range(count)])  55 us
    all_to_all x3, blocking collectives, a2a(): return lax.all_to_all(value, axes, 0, 0, tiled=True)  31.9 us
    pallas_call x2, Pallas kernels, gradient(): pl.pallas_call(kernel, out_shape=[piece(F32)] + [piece(BF)] * 3, grid=(4,...  19.8 us
    all_gather x1, waiting for transfers between devices, on_device(): m_near = lax.all_gather(m, ('z', 'y'), axis=0, tiled=True)  19.7 us
    pallas_call x2, Pallas kernels, project(): pl.pallas_call(project_kernel, out_shape=[jax.ShapeDtypeStruct((2 * tok,...  12.6 us
    ppermute x6, starting transfers between devices, shift_x(): return lax.ppermute(value, ('p', 'h'), pairs)  11 us
    all_to_all x1, starting transfers between devices, a2a(): return lax.all_to_all(value, axes, 0, 0, tiled=True)  8.97 us
  transfers between devices with their start and end apart: 53, of which 27 were waited for; matrix products, arithmetic and copies ran while one was open for 6% of the time, Pallas kernels for 14%

commit v1 on v0

--- a/solution.py
+++ b/solution.py
@@ -1,5 +1,3 @@
-import functools
-
 import jax
 import jax.numpy as jnp
 from jax import lax
@@ -54,49 +52,65 @@
     return (up * s * (1.0 + pre * (1.0 - s))).astype(BF)
 
 
-def cut_kernel(along_z, at_ref, one_ref, two_ref, *outs):
+def cut_kernel(at_ref, x_ref, ct_ref, *outs):
     p, x, c, z, y = (at_ref[i] for i in range(5))
-    tok = one_ref.shape[0]
-    own = one_ref.shape[1] // 16
+    tok = x_ref.shape[0]
+    own = x_ref.shape[1] // 16
     half, part = tok // 2, tok // 8
-    for rc in range(2):
-        for q in range(4):
+
+    def copy(v_ref, u_ref):
+        def group(i, carry):
+            rc, q = i // 4, lax.rem(i, 4)
             source = lax.rem(c + rc, 2) * half + lax.rem(x + 4 - q, 4) * part
             rows = pl.ds(pl.multiple_of(source, part), part)
-            to = rc * half + q * part
+            to = pl.ds(pl.multiple_of(i * part, part), part)
             for k in range(4):
                 for j in range(4):
-                    if along_z:
-                        zz, yy = lax.rem(z + k, 4), lax.rem(y + 4 - j, 4)
-                    else:
-                        zz, yy = lax.rem(z + 4 - j, 4), lax.rem(y + k, 4)
-                    cols = pl.ds(pl.multiple_of((zz * 4 + yy) * own, own), own)
-                    got = jnp.where(p == 0, one_ref[rows, cols], two_ref[rows, cols])
-                    outs[k][to : to + part, j * own : (j + 1) * own] = got
-
-
-def cut(at, one, two, along_z):
-    tok, width = one.shape
+                    at_v = lax.rem(z + k, 4) * 4 + lax.rem(y + 4 - j, 4)
+                    at_u = lax.rem(z + 4 - j, 4) * 4 + lax.rem(y + k, 4)
+                    for out, ref, at in ((outs[k], v_ref, at_v), (outs[4 + k], u_ref, at_u)):
+                        cols = pl.ds(pl.multiple_of(at * own, own), own)
+                        out[to, j * own : (j + 1) * own] = ref[rows, cols]
+            return carry
+
+        lax.fori_loop(0, 8, group, 0)
+
+    @pl.when(p == 0)
+    def _():
+        copy(x_ref, ct_ref)
+
+    @pl.when(p != 0)
+    def _():
+        copy(ct_ref, x_ref)
+
+
+def cut(at, x, ct):
+    tok, width = x.shape
     vmem = pl.BlockSpec(memory_space=pltpu.VMEM)
-    return pl.pallas_call(
-        functools.partial(cut_kernel, along_z),
-        out_shape=[jax.ShapeDtypeStruct((tok, width // 4), BF)] * 4,
+    outs = pl.pallas_call(
+        cut_kernel,
+        out_shape=[jax.ShapeDtypeStruct((tok, width // 4), BF)] * 8,
         in_specs=[pl.BlockSpec(memory_space=pltpu.SMEM), vmem, vmem],
-        out_specs=[vmem] * 4,
-        name="cut_z" if along_z else "cut_y",
-    )(at, one, two)
+        out_specs=[vmem] * 8,
+        name="cut",
+    )(at, x, ct)
+    return list(outs[:4]), list(outs[4:])
 
 
 def project_kernel(*refs):
-    blocks, weights, sent, kept = refs[:4], refs[4:8], refs[8], refs[9]
-    half = blocks[0].shape[0] // 2
-    own = weights[0].shape[0]
-    for rc, out in ((1, sent), (0, kept)):
-        left = jnp.concatenate([b[rc * half : (rc + 1) * half, :] for b in blocks])
-        total = dot(left[:, :own], weights[0][...])
-        for j in range(1, 4):
-            total += dot(left[:, j * own : (j + 1) * own], weights[j][...])
-        out[...] = total.astype(out.dtype)
+    blocks, weights, sent, kept, left = refs[:4], refs[4:8], refs[8], refs[9], refs[10]
+    tok = blocks[0].shape[0]
+    half = tok // 2
+
+    @pl.when(pl.program_id(0) == 0)
+    def _():
+        for k in range(4):
+            left[k * half : (k + 1) * half, :] = blocks[k][half:, :]
+            left[2 * tok + k * half : 2 * tok + (k + 1) * half, :] = blocks[k][:half, :]
+
+    right = jnp.concatenate([w[...] for w in weights])
+    sent[...] = dot(left[: 2 * tok, :], right).astype(BF)
+    kept[...] = dot(left[2 * tok :, :], right)
 
 
 def project(blocks, weights):
@@ -113,6 +127,7 @@
         in_specs=[pl.BlockSpec((tok, wide), lambda n: (0, 0))] * 4
         + [pl.BlockSpec((own, tile), lambda n: (0, n))] * 4,
         out_specs=[pl.BlockSpec((2 * tok, tile), lambda n: (0, n))] * 2,
+        scratch_shapes=[pltpu.VMEM((4 * tok, wide), BF)],
         cost_estimate=pl.CostEstimate(
             flops=8 * tok * wide * hidden, bytes_accessed=8 * tok * wide * 2, transcendentals=0
         ),
@@ -127,27 +142,44 @@
             outs[i][...] = total.astype(outs[i].dtype)
 
 
+def fill(scratch, near, far, part=None):
+    half = near[0].shape[-2]
+    for k in range(4):
+        for i, ref in enumerate((near[k], far[k])):
+            to = (2 * k + i) * half
+            scratch[to : to + half, :] = ref[...] if part is None else ref[part]
+
+
 def grad_v_kernel(*refs):
-    blocks, near, far, outs = refs[:4], refs[4:8], refs[8:12], refs[12:]
-    total = None
-    for k in range(4):
-        right = jnp.concatenate([near[k][...], far[k][...]])
-        term = dot_t0(blocks[k][...], right)
-        total = term if total is None else total + term
-    store_piece(outs, pl.program_id(0), total)
+    blocks, near, far, outs, right = refs[:4], refs[4:8], refs[8:12], refs[12:16], refs[16]
+
+    @pl.when(pl.program_id(0) == 0)
+    def _():
+        fill(right, near, far)
+
+    left = jnp.concatenate([b[...] for b in blocks])
+    store_piece(outs, pl.program_id(0), dot_t0(left, right[...]))
 
 
 def grad_u_kernel(*refs):
-    blocks, near, far = refs[:4], refs[4:8], refs[8:12]
-    w_ref, outs = refs[12], refs[13:]
-    total = None
-    for k in range(4):
-        right = jnp.concatenate([near[k][0], far[k][0]])
-        factor = jnp.concatenate([near[k][1], far[k][1]])
-        left = blocks[k][...].astype(F32) + dot_t1(factor, w_ref[...])
-        term = dot_t0(left.astype(BF), right)
-        total = term if total is None else total + term
-    store_piece(outs, pl.program_id(0), total)
+    blocks, near, far, w_refs = refs[:4], refs[4:8], refs[8:12], refs[12:16]
+    outs, right, factor, fold = refs[16:20], refs[20], refs[21], refs[22]
+    j = pl.program_id(0)
+
+    @pl.when(j == 0)
+    def _():
+        fill(right, near, far, 0)
+        fill(factor, near, far, 1)
+
+    for i in range(4):
+
+        @pl.when(j == i)
+        def _(i=i):
+            fold[...] = w_refs[i][...]
+
+    left = jnp.concatenate([b[...] for b in blocks]).astype(F32)
+    left = (left + dot_t1(factor[...], fold[...])).astype(BF)
+    store_piece(outs, j, dot_t0(left, right[...]))
 
 
 def gradient(kernel, blocks, near, far, weights):
@@ -161,15 +193,17 @@
     def piece(dtype):
         return jax.ShapeDtypeStruct((own, hidden), dtype)
 
-    fold = [pl.BlockSpec((own, hidden), lambda j: (j, 0))] * len(weights)
+    scratch = [pltpu.VMEM((4 * tok, hidden), BF)]
+    if weights:
+        scratch += [pltpu.VMEM((4 * tok, hidden), BF), pltpu.VMEM((own, hidden), BF)]
     return pl.pallas_call(
         kernel,
         out_shape=[piece(F32)] + [piece(BF)] * 3,
         grid=(4,),
         in_specs=[pl.BlockSpec((tok, own), lambda j: (0, j))] * 4
-        + [whole(a) for a in (*near, *far)]
-        + fold,
+        + [whole(a) for a in (*near, *far, *weights)],
         out_specs=[pl.BlockSpec((own, hidden), lambda j: (0, 0))] * 4,
+        scratch_shapes=scratch,
         cost_estimate=pl.CostEstimate(
             flops=8 * tok * wide * hidden, bytes_accessed=8 * tok * wide * 2, transcendentals=0
         ),
@@ -205,20 +239,20 @@
     w_3 = lax.ppermute(w_u, "p", [(0, 1), (1, 0)])
     w_vs = gather(w_v, "y")
     at = jnp.stack([p, h * 2 + p, c, z, y])
-    x = inputs.reshape(tok, cols)
-    ct = cotangent.reshape(tok, cols)
-    vs = list(cut(at, x, ct, True))
-    us = list(cut(at, ct, x, False))
-    vs[0], us[0], w_3 = lax.optimization_barrier((vs[0], us[0], w_3))
+    vs, us = cut(at, inputs.reshape(tok, cols), cotangent.reshape(tok, cols))
     vs = exchange(vs, "z", 1)
     us = exchange(us, "y", 1)
     w_us = gather(w_u, "z")
 
-    m = dot_t0(jnp.where(first, w_u, w_3), jnp.where(first, w_3, w_u))
-    m = lax.dynamic_index_in_dim(m.reshape(2, 16, 2, 2, -1, hidden), p, 2, False)
-    m = m.transpose(1, 2, 0, 3, 4).reshape(hidden // 2, hidden).astype(BF)
-    m = a2a(m, ("z", "y", "h", "c")).reshape(64, -1, hidden)
-    m = m.astype(F32).sum(0).astype(BF)
+    m = 0.0
+    far_u, far_3 = shift(w_u, "c", 1), shift(w_3, "c", 1)
+    for mine_u, mine_3 in ((w_u, w_3), (far_u, far_3)):
+        m += dot_t0(jnp.where(first, mine_u, mine_3), jnp.where(first, mine_3, mine_u))
+    m = lax.dynamic_slice(
+        m.reshape(2, 16, 2, -1, hidden), (c, 0, p, 0, 0), (1, 16, 1, hidden // 64, hidden)
+    )
+    m = a2a(m.reshape(hidden // 4, hidden).astype(BF), ("z", "y", "h"))
+    m = m.reshape(32, -1, hidden).astype(F32).sum(0).astype(BF)
     m = a2a(jnp.broadcast_to(m[None], (4,) + m.shape), ("p", "h")).reshape(-1, hidden)
     w_us[0], m = lax.optimization_barrier((w_us[0], m))
     m_near = lax.all_gather(m, ("z", "y"), axis=0, tiled=True)
@@ -231,8 +265,7 @@
 
     a_v = reduced(vs, w_vs, "z")
     a_u = reduced(us, w_us, "y")
-    a_u, a_v, w_3 = lax.optimization_barrier((a_u, a_v, w_3))
-    w_3 = jnp.concatenate(gather(w_3, "z"))
+    w_3s = gather(w_3, "z")
 
     both = jnp.concatenate([a_u, a_v], 1)
     pieces = [both[(4 - k) % 4 * mine :][:mine] for k in range(4)]
@@ -266,7 +299,7 @@
     pq_far = [shift(a, "c", 1) for a in pq_near]
 
     g_v = sum_back(gradient(grad_v_kernel, vs, r_near, r_far, ()), "y")
-    g_u = sum_back(gradient(grad_u_kernel, us, pq_near, pq_far, (w_3,)), "z")
+    g_u = sum_back(gradient(grad_u_kernel, us, pq_near, pq_far, w_3s), "z")
 
     squares = jnp.sum(g_u * g_u) + jnp.sum(g_v * g_v)
     for axes, count in ((("z", "y"), 16), (("p", "h", "c"), 8)):

time: 300 us -> 295 us (0.983)
  starting transfers between devices: 76.6 us -> 63.7 us
  waiting for transfers between devices: 99.6 us -> 111 us
    ppermute x44 -> x46, waiting for transfers between devices: 73.9 us -> 85.2 us  [shift(): lax.ppermute(value, axis, [(i, (i + by) % count) for i in range(count)])]
    ppermute x44 -> x46, starting transfers between devices: 55 us -> 45.3 us  [shift(): lax.ppermute(value, axis, [(i, (i + by) % count) for i in range(count)])]
    all_gather x1, waiting for transfers between devices: 19.7 us -> 16.5 us  [on_device(): m_near = lax.all_gather(m, ('z', 'y'), axis=0, tiled=True)]
    pallas_call x2 -> x1, Pallas kernels: 8.18 us -> 5.05 us  [cut(): pl.pallas_call(cut_kernel, out_shape=[jax.ShapeDtypeStruct((tok, width //...]
    unnamed x58 -> x52, local copies, waits for them, and re-layouts: 8.67 us -> 7.64 us
  transfers between devices with their start and end apart: 53 -> 55, of which waited for: 27 -> 26; matrix products, arithmetic and copies ran while one was open for 6% -> 5% of each run, Pallas kernels for 14% -> 14%
where the time goes in v1:
time: 295 us; the launch traced here: 293 us
  waiting for transfers between devices  111 us (38%)
  starting transfers between devices  63.7 us (22%)
  Pallas kernels  39.6 us (13%)
  blocking collectives  31.8 us (11%)
  between operations  17.6 us (6%)
  other arithmetic  15.8 us (5%)
  local copies, waits for them, and re-layouts  10.8 us (4%)
  matrix products  2.99 us (1%)
    ppermute x46, waiting for transfers between devices, shift(): lax.ppermute(value, axis, [(i, (i + by) % count) for i in range(count)])  85.2 us
    ppermute x46, starting transfers between devices, shift(): lax.ppermute(value, axis, [(i, (i + by) % count) for i in range(count)])  45.3 us
    all_to_all x3, blocking collectives, a2a(): return lax.all_to_all(value, axes, 0, 0, tiled=True)  31.8 us
    pallas_call x2, Pallas kernels, gradient(): pl.pallas_call(kernel, out_shape=[piece(F32)] + [piece(BF)] * 3, grid=(4,...  21.7 us
    all_gather x1, waiting for transfers between devices, on_device(): m_near = lax.all_gather(m, ('z', 'y'), axis=0, tiled=True)  16.5 us
    pallas_call x2, Pallas kernels, project(): pl.pallas_call(project_kernel, out_shape=[jax.ShapeDtypeStruct((2 * tok,...  12.9 us
    ppermute x6, starting transfers between devices, shift_x(): return lax.ppermute(value, ('p', 'h'), pairs)  10.1 us
    unnamed x52, local copies, waits for them, and re-layouts  7.64 us
  transfers between devices with their start and end apart: 55, of which 26 were waited for; matrix products, arithmetic and copies ran while one was open for 5% of the time, Pallas kernels for 14%

profile of v1, /device:TPU:0, one launch (start us, length us, event | category | flops | bytes accessed | tf_op | source)
XLA Modules:
  0.0 293.3 jit_solution(469427718961613083)
XLA Ops:
  8.4 1.9 bitcast_select_fusion.1
  12.6 5.0 %cut.1 = (bf16[256,1024]{1,0:T(8,128)(2,1)}, bf16[256,1024]{1,0:T(8,128)(2,1)}, bf16[256,1024]{1,0:T(8,128)(2,1)}, bf16[256,1024]{1,0:T(8,128)(2,1)}, bf16[256,1...) custom-call(s32[5]{0:T(128)} %stack.43.at_ref, ...), custom_call_target="tpu_custom_call" | custom-call | tf_op jit(solution)/shard_map/cut/pallas_call | solution.py:90
  19.2 1.9 collective-permute-start
  21.2 3.6 %collective-permute-start.1 = (bf16[256,1024]{1,0:T(8,128)(2,1)}, bf16[256,1024]{1,0:T(8,128)(2,1)}, u32[]{:S(2)}, u32[]{:S(2)}) collective-permute-start(bf16[256,1024]{1,0:T(8,128)(2,1)} %get-tuple-element.27), channel_id=1, source_target_pairs={{0,8},{4,12},{8,0},{12,4},{1,9},{5,13},{9,1},{13,5},{2,10},{6,14},... | collective-permute-start | bytes 1572872 | tf_op jit(solution)/shard_map/ppermute | solution.py:34
  27.2 6.7 %collective-permute-done.3.refs_1_ = bf16[256,1024]{1,0:T(8,128)(2,1)S(1)} collective-permute-done((bf16[256,1024]{1,0:T(8,128)(2,1)}, bf16[256,1024]{1,0:T(8,128)(2,1)S(1)}, u32[]{:S(2)}, u32[]{:S(2)}) %collective-permute-start.3) | collective-permute-done | bytes 524320 | tf_op jit(solution)/shard_map/ppermute | solution.py:34
  33.9 2.0 collective-permute-start.17
  37.5 10.8 %collective-permute-done.1.refs_2_ = bf16[256,1024]{1,0:T(8,128)(2,1)} collective-permute-done((bf16[256,1024]{1,0:T(8,128)(2,1)}, bf16[256,1024]{1,0:T(8,128)(2,1)}, u32[]{:S(2)}, u32[]{:S(2)}) %collective-permute-start.1) | collective-permute-done | bytes 524320 | tf_op jit(solution)/shard_map/ppermute | solution.py:34
  48.3 2.9 collective-permute-start.4
  52.9 6.6 %all-to-all-start = ((bf16[32,8,1024]{2,1,0:T(8,128)(2,1)}), bf16[32,8,1024]{2,1,0:T(8,128)(2,1)S(1)}, u32[]{:S(2)}, u32[]{:S(2)}) async-start(bf16[32,8,1024]{2,1,0:T(8,128)(2,1)} %bitcast.11), calls=%async_computation | async-start | bytes 1048576 | tf_op jit(solution)/shard_map/all_to_all | solution.py:29
  59.6 5.6 %collective-permute-done.2.refs_3_ = bf16[256,1024]{1,0:T(8,128)(2,1)} collective-permute-done((bf16[256,1024]{1,0:T(8,128)(2,1)}, bf16[256,1024]{1,0:T(8,128)(2,1)}, u32[]{:S(2)}, u32[]{:S(2)}) %collective-permute-start.2) | collective-permute-done | bytes 524320 | tf_op jit(solution)/shard_map/ppermute | solution.py:34
  65.2 1.9 collective-permute-start.11
  68.9 6.4 %shard_map.68 = (bf16[512,1024]{1,0:T(8,128)(2,1)}, f32[512,1024]{1,0:T(8,128)}) custom-call(bf16[256,1024]{1,0:T(8,128)(2,1)} %get-tuple-element.25.refs_0_, bf16[256,1024]{1,0:T(8,128)(2,1)} %copy-done.18, bf16[256,1024]{1,0:T(8,128)(2,1)} %collective-permute-done.1.refs_2_, bf16[256,1024]{1,0:T(8,128)(2,1)} %collective-permute-done.2.refs_3_, ...), custom_call_target="tpu_custom_call" | custom-call | flops 2147483648 | bytes 4194304 | tf_op jit(solution)/shard_map/pallas_call | solution.py:120
  76.1 2.8 all-to-all-done
  79.1 9.3 %all_to_all.21 = bf16[4,8,1024]{2,1,0:T(8,128)(2,1)} all-to-all(bf16[4,8,1024]{2,1,0:T(8,128)(2,1)S(1)} %broadcast_in_dim.18), channel_id=1, replica_groups=mesh['p'=2,'h'=2,'c'=2,'z'=4,'y'=4] {'p','h'}, dimensions={0} | all-to-all | bytes 131072 | tf_op jit(solution)/shard_map/all_to_all | solution.py:29
  88.3 4.9 %collective-permute-done.11.refs_7_ = bf16[256,1024]{1,0:T(8,128)(2,1)} collective-permute-done((bf16[256,1024]{1,0:T(8,128)(2,1)S(1)}, bf16[256,1024]{1,0:T(8,128)(2,1)}, u32[]{:S(2)}, u32[]{:S(2)}) %collective-permute-start.11) | collective-permute-done | bytes 524320 | tf_op jit(solution)/shard_map/ppermute | solution.py:34
  93.8 6.4 %shard_map.67 = (bf16[512,1024]{1,0:T(8,128)(2,1)}, f32[512,1024]{1,0:T(8,128)}) custom-call(bf16[256,1024]{1,0:T(8,128)(2,1)} %get-tuple-element.29.refs_0_, bf16[256,1024]{1,0:T(8,128)(2,1)} %copy-done.7, bf16[256,1024]{1,0:T(8,128)(2,1)} %copy-done.8, bf16[256,1024]{1,0:T(8,128)(2,1)} %copy-done.9, bf16[256,1024]{1,0:T(8,128)(2,1)} %copy-done.1, ...), custom_call_target="tpu_custom_call" | custom-call | flops 2147483648 | bytes 4194304 | tf_op jit(solution)/shard_map/pallas_call | solution.py:120
  101.3 2.3 fusion.37
  104.5 2.1 collective-permute-start.20
  106.5 2.6 collective-permute-start.21
  110.6 2.3 fusion.36
  113.3 5.8 %collective-permute-done.20 = bf16[128,1024]{1,0:T(8,128)(2,1)S(1)} collective-permute-done((bf16[128,1024]{1,0:T(8,128)(2,1)}, bf16[128,1024]{1,0:T(8,128)(2,1)S(1)}, u32[]{:S(2)}, u32[]{:S(2)}) %collective-permute-start.20) | collective-permute-done | bytes 262176 | tf_op jit(solution)/shard_map/ppermute | solution.py:34
  119.1 3.6 %collective-permute-done.22 = bf16[128,1024]{1,0:T(8,128)(2,1)S(1)} collective-permute-done((bf16[128,1024]{1,0:T(8,128)(2,1)}, bf16[128,1024]{1,0:T(8,128)(2,1)S(1)}, u32[]{:S(2)}, u32[]{:S(2)}) %collective-permute-start.22) | collective-permute-done | bytes 262176 | tf_op jit(solution)/shard_map/ppermute | solution.py:34
  124.5 4.7 %collective-permute-done.15 = bf16[128,1024]{1,0:T(8,128)(2,1)S(1)} collective-permute-done((bf16[128,1024]{1,0:T(8,128)(2,1)S(1)}, bf16[128,1024]{1,0:T(8,128)(2,1)S(1)}, u32[]{:S(2)}, u32[]{:S(2)}) %collective-permute-start.15) | collective-permute-done | bytes 262176 | tf_op jit(solution)/shard_map/ppermute | solution.py:34
  131.6 2.6 collective-permute-start.25
  134.6 16.5 %all-gather.2.cloned.1.call-done = bf16[512,1024]{1,0:T(8,128)(2,1)} async-done(((bf16[32,1024]{1,0:T(8,128)(2,1)}), bf16[512,1024]{1,0:T(8,128)(2,1)}) %all-gather.2.cloned.1.call-update) | async-done | bytes 1048592 | tf_op jit(solution)/shard_map/all_gather | solution.py:258
  156.6 2.6 collective-permute-start.28
  163.7 4.6 %collective-permute-done.28 = bf16[3,32,1024]{2,1,0:T(8,128)(2,1)S(1)} collective-permute-done((bf16[3,32,1024]{2,1,0:T(8,128)(2,1)S(1)}, bf16[3,32,1024]{2,1,0:T(8,128)(2,1)S(1)}, u32[]{:S(2)}, u32[]{:S(2)}) %collective-permute-start.28) | collective-permute-done | bytes 196640 | tf_op jit(solution)/shard_map/ppermute | solution.py:43
  169.6 2.5 collective-permute-start.31
  172.6 2.1 collective-permute-start.41
  174.7 2.4 collective-permute-done.48.refs_14_
  177.1 1.9 collective-permute-start.42
  179.0 3.7 %collective-permute-done.30.refs_5_ = bf16[128,1024]{1,0:T(8,128)(2,1)S(1)} collective-permute-done((bf16[128,1024]{1,0:T(8,128)(2,1)S(1)}, bf16[128,1024]{1,0:T(8,128)(2,1)S(1)}, u32[]{:S(2)}, u32[]{:S(2)}) %collective-permute-start.30) | collective-permute-done | bytes 262176 | tf_op jit(solution)/shard_map/ppermute | solution.py:34
  183.3 3.4 %collective-permute-done.31.refs_6_ = bf16[128,1024]{1,0:T(8,128)(2,1)S(1)} collective-permute-done((bf16[128,1024]{1,0:T(8,128)(2,1)S(1)}, bf16[128,1024]{1,0:T(8,128)(2,1)S(1)}, u32[]{:S(2)}, u32[]{:S(2)}) %collective-permute-start.31) | collective-permute-done | bytes 262176 | tf_op jit(solution)/shard_map/ppermute | solution.py:34
  186.7 4.1 %collective-permute-done.32.refs_7_ = bf16[128,1024]{1,0:T(8,128)(2,1)S(1)} collective-permute-done((bf16[128,1024]{1,0:T(8,128)(2,1)S(1)}, bf16[128,1024]{1,0:T(8,128)(2,1)S(1)}, u32[]{:S(2)}, u32[]{:S(2)}) %collective-permute-start.32) | collective-permute-done | bytes 262176 | tf_op jit(solution)/shard_map/ppermute | solution.py:34
  192.4 4.7 %collective-permute-done.40.refs_5_ = bf16[2,128,1024]{2,1,0:T(8,128)(2,1)S(1)} collective-permute-done((bf16[2,128,1024]{2,1,0:T(8,128)(2,1)S(1)}, bf16[2,128,1024]{2,1,0:T(8,128)(2,1)S(1)}, u32[]{:S(2)}, u32[]{:S(2)}) %collective-permute-start.40) | collective-permute-done | bytes 524320 | tf_op jit(solution)/shard_map/ppermute | solution.py:34
  200.1 7.0 %shard_map.69 = (f32[256,1024]{1,0:T(8,128)}, bf16[256,1024]{1,0:T(8,128)(2,1)}, bf16[256,1024]{1,0:T(8,128)(2,1)}, bf16[256,1024]{1,0:T(8,128)(2,1)}) custom-call(bf16[256,1024]{1,0:T(8,128)(2,1)} %get-tuple-element.25.refs_0_, bf16[256,1024]{1,0:T(8,128)(2,1)} %copy-done.18, bf16[256,1024]{1,0:T(8,128)(2,1)} %collective-permute-done.1.refs_2_, ...), custom_call_target="tpu_custom_call" | custom-call | flops 2147483648 | bytes 4194304 | tf_op jit(solution)/shard_map/pallas_call | solution.py:199
  207.2 2.4 collective-permute-start.37
  210.9 14.7 %shard_map.70 = (f32[256,1024]{1,0:T(8,128)}, bf16[256,1024]{1,0:T(8,128)(2,1)}, bf16[256,1024]{1,0:T(8,128)(2,1)}, bf16[256,1024]{1,0:T(8,128)(2,1)}) custom-call(bf16[256,1024]{1,0:T(8,128)(2,1)} %get-tuple-element.29.refs_0_, bf16[256,1024]{1,0:T(8,128)(2,1)} %copy-done.7, bf16[256,1024]{1,0:T(8,128)(2,1)} %copy-done.8, bf16[256,1024]{1,0:T(8,128)(2,1)} %copy-done.9, ...), custom_call_target="tpu_custom_call" | custom-call | flops 2147483648 | bytes 4194304 | tf_op jit(solution)/shard_map/pallas_call | solution.py:199
  228.3 4.7 %collective-permute-done.37 = bf16[256,1024]{1,0:T(8,128)(2,1)S(1)} collective-permute-done((bf16[256,1024]{1,0:T(8,128)(2,1)}, bf16[256,1024]{1,0:T(8,128)(2,1)S(1)}, u32[]{:S(2)}, u32[]{:S(2)}) %collective-permute-start.37) | collective-permute-done | bytes 524320 | tf_op jit(solution)/shard_map/ppermute | solution.py:34
  233.6 3.0 %collective-permute-done.39 = bf16[256,1024]{1,0:T(8,128)(2,1)S(1)} collective-permute-done((bf16[256,1024]{1,0:T(8,128)(2,1)}, bf16[256,1024]{1,0:T(8,128)(2,1)S(1)}, u32[]{:S(2)}, u32[]{:S(2)}) %collective-permute-start.39) | collective-permute-done | bytes 524320 | tf_op jit(solution)/shard_map/ppermute | solution.py:34
  236.6 2.0 multiply_reduce_fusion
  238.5 2.1 collective-permute-done.50
  240.6 2.6 collective-permute-done.51
  243.2 9.9 %collective-permute-done.52 = bf16[256,1024]{1,0:T(8,128)(2,1)S(1)} collective-permute-done((bf16[256,1024]{1,0:T(8,128)(2,1)}, bf16[256,1024]{1,0:T(8,128)(2,1)S(1)}, u32[]{:S(2)}, u32[]{:S(2)}) %collective-permute-start.52) | collective-permute-done | bytes 524320 | tf_op jit(solution)/shard_map/ppermute | solution.py:34
  253.1 1.9 multiply_reduce_fusion.1
  256.3 12.8 %all_to_all.22 = f32[16,8,128]{2,1,0:T(8,128)S(1)} all-to-all(f32[16,8,128]{2,1,0:T(8,128)S(1)} %broadcast_in_dim.19), channel_id=1, replica_groups=mesh['p'=2,'h'=2,'c'=2,'z'=4,'y'=4] {'z','y'}, dimensions={0} | all-to-all | bytes 131072 | tf_op jit(solution)/shard_map/all_to_all | solution.py:29
  270.4 9.8 %all_to_all.23 = f32[8,8,128]{2,1,0:T(8,128)S(1)} all-to-all(f32[8,8,128]{2,1,0:T(8,128)S(1)} %broadcast_in_dim.20), channel_id=1, replica_groups=mesh['p'=2,'h'=2,'c'=2,'z'=4,'y'=4] {'p','h','c'}, dimensions={0} | all-to-all | bytes 65536 | tf_op jit(solution)/shard_map/all_to_all | solution.py:29
  281.5 2.5 multiply_bitcast_fusion
  (156 shorter events, 47.3 us)
Async XLA Ops:
  10.3 14.4 %collective-permute-start.6 = (bf16[256,1024]{1,0:T(8,128)(2,1)S(1)}, bf16[256,1024]{1,0:T(8,128)(2,1)S(1)}, u32[]{:S(2)}, u32[]{:S(2)}) collective-permute-start(bf16[256,1024]{1,0:T(8,128)(2,1)S(1)} %get-tuple-element.33.refs_4_), channel_id=1, source_target_pairs={{0,64},{64,0},{1,65},{65,1},{2,66},{66,2},{3,67},{67,3},{4,68},{68... | collective-permute-start | bytes 1572872 | tf_op jit(solution)/shard_map/ppermute | solution.py:239
  12.0 13.6 %collective-permute-start.7 = (bf16[256,1024]{1,0:T(8,128)(2,1)S(1)}, bf16[256,1024]{1,0:T(8,128)(2,1)S(1)}, u32[]{:S(2)}, u32[]{:S(2)}) collective-permute-start(bf16[256,1024]{1,0:T(8,128)(2,1)S(1)} %get-tuple-element.33.refs_4_), channel_id=1, source_target_pairs={{0,16},{16,0},{1,17},{17,1},{2,18},{18,2},{3,19},{19,3},{4,20},{20... | collective-permute-start | bytes 1572872 | tf_op jit(solution)/shard_map/ppermute | solution.py:34
  17.7 16.2 %collective-permute-start.3 = (bf16[256,1024]{1,0:T(8,128)(2,1)}, bf16[256,1024]{1,0:T(8,128)(2,1)S(1)}, u32[]{:S(2)}, u32[]{:S(2)}) collective-permute-start(bf16[256,1024]{1,0:T(8,128)(2,1)} %get-tuple-element.30), channel_id=1, source_target_pairs={{0,1},{1,2},{2,3},{3,0},{4,5},{5,6},{6,7},{7,4},{8,9},{9,10},{10,1... | collective-permute-start | bytes 1572872 | tf_op jit(solution)/shard_map/ppermute | solution.py:34
  19.2 16.6 %collective-permute-start = (bf16[256,1024]{1,0:T(8,128)(2,1)}, bf16[256,1024]{1,0:T(8,128)(2,1)S(1)}, u32[]{:S(2)}, u32[]{:S(2)}) collective-permute-start(bf16[256,1024]{1,0:T(8,128)(2,1)} %get-tuple-element.26), channel_id=1, source_target_pairs={{0,4},{4,8},{8,12},{12,0},{1,5},{5,9},{9,13},{13,1},{2,6},{6,10},{... | collective-permute-start | bytes 1572872 | tf_op jit(solution)/shard_map/ppermute | solution.py:34
  21.2 27.2 %collective-permute-start.1 = (bf16[256,1024]{1,0:T(8,128)(2,1)}, bf16[256,1024]{1,0:T(8,128)(2,1)}, u32[]{:S(2)}, u32[]{:S(2)}) collective-permute-start(bf16[256,1024]{1,0:T(8,128)(2,1)} %get-tuple-element.27), channel_id=1, source_target_pairs={{0,8},{4,12},{8,0},{12,4},{1,9},{5,13},{9,1},{13,5},{2,10},{6,14},... | collective-permute-start | bytes 1572872 | tf_op jit(solution)/shard_map/ppermute | solution.py:34
  24.8 26.5 %collective-permute-start.8 = (bf16[256,1024]{1,0:T(8,128)(2,1)S(1)}, bf16[256,1024]{1,0:T(8,128)(2,1)S(1)}, u32[]{:S(2)}, u32[]{:S(2)}) collective-permute-start(bf16[256,1024]{1,0:T(8,128)(2,1)S(1)} %collective-permute-done.6.refs_12_), channel_id=1, source_target_pairs={{0,16},{16,0},{1,17},{17,1},{2,18},{18,2},{3,19},{19,3},{4,20},{20... | collective-permute-start | bytes 1572872 | tf_op jit(solution)/shard_map/ppermute | solution.py:34
  25.5 39.6 %collective-permute-start.16 = (bf16[256,1024]{1,0:T(8,128)(2,1)}, bf16[256,1024]{1,0:T(8,128)(2,1)}, u32[]{:S(2)}, u32[]{:S(2)}) collective-permute-start(bf16[256,1024]{1,0:T(8,128)(2,1)} %get-tuple-element.72.refs_4_), channel_id=1, source_target_pairs={{0,1},{1,2},{2,3},{3,0},{4,5},{5,6},{6,7},{7,4},{8,9},{9,10},{10,1... | collective-permute-start | bytes 1572872 | tf_op jit(solution)/shard_map/ppermute | solution.py:34
  33.9 33.2 %collective-permute-start.17 = (bf16[256,1024]{1,0:T(8,128)(2,1)}, bf16[256,1024]{1,0:T(8,128)(2,1)}, u32[]{:S(2)}, u32[]{:S(2)}) collective-permute-start(bf16[256,1024]{1,0:T(8,128)(2,1)} %get-tuple-element.72.refs_4_), channel_id=1, source_target_pairs={{0,2},{1,3},{2,0},{3,1},{4,6},{5,7},{6,4},{7,5},{8,10},{9,11},{10,... | collective-permute-start | bytes 1572872 | tf_op jit(solution)/shard_map/ppermute | solution.py:34
  35.9 31.4 %collective-permute-start.18 = (bf16[256,1024]{1,0:T(8,128)(2,1)}, bf16[256,1024]{1,0:T(8,128)(2,1)}, u32[]{:S(2)}, u32[]{:S(2)}) collective-permute-start(bf16[256,1024]{1,0:T(8,128)(2,1)} %get-tuple-element.72.refs_4_), channel_id=1, source_target_pairs={{0,3},{1,0},{2,1},{3,2},{4,7},{5,4},{6,5},{7,6},{8,11},{9,8},{10,9... | collective-permute-start | bytes 1572872 | tf_op jit(solution)/shard_map/ppermute | solution.py:34
  48.3 27.0 %collective-permute-start.4 = (bf16[256,1024]{1,0:T(8,128)(2,1)}, bf16[256,1024]{1,0:T(8,128)(2,1)S(1)}, u32[]{:S(2)}, u32[]{:S(2)}) collective-permute-start(bf16[256,1024]{1,0:T(8,128)(2,1)} %get-tuple-element.31), channel_id=1, source_target_pairs={{0,2},{1,3},{2,0},{3,1},{4,6},{5,7},{6,4},{7,5},{8,10},{9,11},{10,... | collective-permute-start | bytes 1572872 | tf_op jit(solution)/shard_map/ppermute | solution.py:34
  51.2 13.9 %collective-permute-start.2 = (bf16[256,1024]{1,0:T(8,128)(2,1)}, bf16[256,1024]{1,0:T(8,128)(2,1)}, u32[]{:S(2)}, u32[]{:S(2)}) collective-permute-start(bf16[256,1024]{1,0:T(8,128)(2,1)} %get-tuple-element.28), channel_id=1, source_target_pairs={{0,12},{4,0},{8,4},{12,8},{1,13},{5,1},{9,5},{13,9},{2,14},{6,2},{... | collective-permute-start | bytes 1572872 | tf_op jit(solution)/shard_map/ppermute | solution.py:34
  52.9 26.1 %all-to-all-start = ((bf16[32,8,1024]{2,1,0:T(8,128)(2,1)}), bf16[32,8,1024]{2,1,0:T(8,128)(2,1)S(1)}, u32[]{:S(2)}, u32[]{:S(2)}) async-start(bf16[32,8,1024]{2,1,0:T(8,128)(2,1)} %bitcast.11), calls=%async_computation | async-start | bytes 1048576 | tf_op jit(solution)/shard_map/all_to_all | solution.py:29
  59.5 91.5 %all-gather.2.cloned.1.call-start = ((), (), s32[]{:S(2)}) async-start(), calls=%async_computation.4 | async-start | bytes 1114112 | tf_op jit(solution)/shard_map/all_gather | solution.py:258
  65.2 23.2 %collective-permute-start.10 = (bf16[256,1024]{1,0:T(8,128)(2,1)S(1)}, bf16[256,1024]{1,0:T(8,128)(2,1)}, u32[]{:S(2)}, u32[]{:S(2)}) collective-permute-start(bf16[256,1024]{1,0:T(8,128)(2,1)S(1)} %get-tuple-element.33.refs_4_), channel_id=1, source_target_pairs={{0,8},{4,12},{8,0},{12,4},{1,9},{5,13},{9,1},{13,5},{2,10},{6,14},... | collective-permute-start | bytes 1572872 | tf_op jit(solution)/shard_map/ppermute | solution.py:34
  65.2 28.1 %collective-permute-start.11 = (bf16[256,1024]{1,0:T(8,128)(2,1)S(1)}, bf16[256,1024]{1,0:T(8,128)(2,1)}, u32[]{:S(2)}, u32[]{:S(2)}) collective-permute-start(bf16[256,1024]{1,0:T(8,128)(2,1)S(1)} %get-tuple-element.33.refs_4_), channel_id=1, source_target_pairs={{0,12},{4,0},{8,4},{12,8},{1,13},{5,1},{9,5},{13,9},{2,14},{6,2},{... | collective-permute-start | bytes 1572872 | tf_op jit(solution)/shard_map/ppermute | solution.py:34
  67.1 26.8 %collective-permute-start.9 = (bf16[256,1024]{1,0:T(8,128)(2,1)S(1)}, bf16[256,1024]{1,0:T(8,128)(2,1)}, u32[]{:S(2)}, u32[]{:S(2)}) collective-permute-start(bf16[256,1024]{1,0:T(8,128)(2,1)S(1)} %get-tuple-element.33.refs_4_), channel_id=1, source_target_pairs={{0,4},{4,8},{8,12},{12,0},{1,5},{5,9},{9,13},{13,1},{2,6},{6,10},{... | collective-permute-start | bytes 1572872 | tf_op jit(solution)/shard_map/ppermute | solution.py:34
  67.3 21.1 %collective-permute-start.5 = (bf16[256,1024]{1,0:T(8,128)(2,1)}, bf16[256,1024]{1,0:T(8,128)(2,1)S(1)}, u32[]{:S(2)}, u32[]{:S(2)}) collective-permute-start(bf16[256,1024]{1,0:T(8,128)(2,1)} %get-tuple-element.32), channel_id=1, source_target_pairs={{0,3},{1,0},{2,1},{3,2},{4,7},{5,4},{6,5},{7,6},{8,11},{9,8},{10,9... | collective-permute-start | bytes 1572872 | tf_op jit(solution)/shard_map/ppermute | solution.py:34
  76.1 24.2 %collective-permute-start.19 = (bf16[512,1024]{1,0:T(8,128)(2,1)}, bf16[512,1024]{1,0:T(8,128)(2,1)S(1)}, u32[]{:S(2)}, u32[]{:S(2)}) collective-permute-start(bf16[512,1024]{1,0:T(8,128)(2,1)} %get-tuple-element.37), channel_id=1, source_target_pairs={{0,16},{16,0},{1,17},{17,1},{2,18},{18,2},{3,19},{19,3},{4,20},{20... | collective-permute-start | bytes 3145736 | tf_op jit(solution)/shard_map/ppermute | solution.py:34
  100.3 10.3 %collective-permute-start.12 = (bf16[512,1024]{1,0:T(8,128)(2,1)}, bf16[512,1024]{1,0:T(8,128)(2,1)}, u32[]{:S(2)}, u32[]{:S(2)}) collective-permute-start(bf16[512,1024]{1,0:T(8,128)(2,1)} %get-tuple-element.35), channel_id=1, source_target_pairs={{0,16},{16,0},{1,17},{17,1},{2,18},{18,2},{3,19},{19,3},{4,20},{20... | collective-permute-start | bytes 3145736 | tf_op jit(solution)/shard_map/ppermute | solution.py:34
  104.5 14.6 %collective-permute-start.20 = (bf16[128,1024]{1,0:T(8,128)(2,1)}, bf16[128,1024]{1,0:T(8,128)(2,1)S(1)}, u32[]{:S(2)}, u32[]{:S(2)}) collective-permute-start(bf16[128,1024]{1,0:T(8,128)(2,1)} %get-tuple-element.73), channel_id=1, source_target_pairs={{0,12},{4,0},{8,4},{12,8},{1,13},{5,1},{9,5},{13,9},{2,14},{6,2},{... | collective-permute-start | bytes 786440 | tf_op jit(solution)/shard_map/ppermute | solution.py:34
  106.5 12.5 %collective-permute-start.21 = (bf16[128,1024]{1,0:T(8,128)(2,1)}, bf16[128,1024]{1,0:T(8,128)(2,1)S(1)}, u32[]{:S(2)}, u32[]{:S(2)}) collective-permute-start(bf16[128,1024]{1,0:T(8,128)(2,1)} %get-tuple-element.75), channel_id=1, source_target_pairs={{0,8},{4,12},{8,0},{12,4},{1,9},{5,13},{9,1},{13,5},{2,10},{6,14},... | collective-permute-start | bytes 786440 | tf_op jit(solution)/shard_map/ppermute | solution.py:34
  109.2 13.5 %collective-permute-start.22 = (bf16[128,1024]{1,0:T(8,128)(2,1)}, bf16[128,1024]{1,0:T(8,128)(2,1)S(1)}, u32[]{:S(2)}, u32[]{:S(2)}) collective-permute-start(bf16[128,1024]{1,0:T(8,128)(2,1)} %get-tuple-element.74), channel_id=1, source_target_pairs={{0,4},{4,8},{8,12},{12,0},{1,5},{5,9},{9,13},{13,1},{2,6},{6,10},{... | collective-permute-start | bytes 786440 | tf_op jit(solution)/shard_map/ppermute | solution.py:34
  112.9 11.6 %collective-permute-start.13 = (bf16[128,1024]{1,0:T(8,128)(2,1)S(1)}, bf16[128,1024]{1,0:T(8,128)(2,1)S(1)}, u32[]{:S(2)}, u32[]{:S(2)}) collective-permute-start(bf16[128,1024]{1,0:T(8,128)(2,1)S(1)} %get-tuple-element.68), channel_id=1, source_target_pairs={{0,3},{1,0},{2,1},{3,2},{4,7},{5,4},{6,5},{7,6},{8,11},{9,8},{10,9... | collective-permute-start | bytes 786440 | tf_op jit(solution)/shard_map/ppermute | solution.py:34
  113.2 11.3 %collective-permute-start.14 = (bf16[128,1024]{1,0:T(8,128)(2,1)S(1)}, bf16[128,1024]{1,0:T(8,128)(2,1)S(1)}, u32[]{:S(2)}, u32[]{:S(2)}) collective-permute-start(bf16[128,1024]{1,0:T(8,128)(2,1)S(1)} %get-tuple-element.70), channel_id=1, source_target_pairs={{0,2},{1,3},{2,0},{3,1},{4,6},{5,7},{6,4},{7,5},{8,10},{9,11},{10,... | collective-permute-start | bytes 786440 | tf_op jit(solution)/shard_map/ppermute | solution.py:34
  119.1 10.2 %collective-permute-start.15 = (bf16[128,1024]{1,0:T(8,128)(2,1)S(1)}, bf16[128,1024]{1,0:T(8,128)(2,1)S(1)}, u32[]{:S(2)}, u32[]{:S(2)}) collective-permute-start(bf16[128,1024]{1,0:T(8,128)(2,1)S(1)} %get-tuple-element.69), channel_id=1, source_target_pairs={{0,1},{1,2},{2,3},{3,0},{4,5},{5,6},{6,7},{7,4},{8,9},{9,10},{10,1... | collective-permute-start | bytes 786440 | tf_op jit(solution)/shard_map/ppermute | solution.py:34
  129.5 21.6 %collective-permute-start.23 = (bf16[32,2048]{1,0:T(8,128)(2,1)S(1)}, bf16[32,2048]{1,0:T(8,128)(2,1)S(1)}, u32[]{:S(2)}, u32[]{:S(2)}) collective-permute-start(bf16[32,2048]{1,0:T(8,128)(2,1)S(1)} %get-tuple-element.76), channel_id=1, source_target_pairs={{0,32},{32,0},{64,96},{96,64},{1,33},{33,1},{65,97},{97,65},{2,34}... | collective-permute-start | bytes 393224 | tf_op jit(solution)/shard_map/ppermute | solution.py:43
  130.9 20.2 %collective-permute-start.24 = (bf16[32,2048]{1,0:T(8,128)(2,1)S(1)}, bf16[32,2048]{1,0:T(8,128)(2,1)S(1)}, u32[]{:S(2)}, u32[]{:S(2)}) collective-permute-start(bf16[32,2048]{1,0:T(8,128)(2,1)S(1)} %get-tuple-element.78), channel_id=1, source_target_pairs={{0,64},{32,96},{64,32},{96,0},{1,65},{33,97},{65,33},{97,1},{2,66}... | collective-permute-start | bytes 393224 | tf_op jit(solution)/shard_map/ppermute | solution.py:43
  131.6 19.5 %collective-permute-start.25 = (bf16[32,2048]{1,0:T(8,128)(2,1)S(1)}, bf16[32,2048]{1,0:T(8,128)(2,1)S(1)}, u32[]{:S(2)}, u32[]{:S(2)}) collective-permute-start(bf16[32,2048]{1,0:T(8,128)(2,1)S(1)} %get-tuple-element.77), channel_id=1, source_target_pairs={{0,96},{32,64},{64,0},{96,32},{1,97},{33,65},{65,1},{97,33},{2,98}... | collective-permute-start | bytes 393224 | tf_op jit(solution)/shard_map/ppermute | solution.py:43
  134.1 38.5 %collective-permute-start.47 = (bf16[256,1024]{1,0:T(8,128)(2,1)S(1)}, bf16[256,1024]{1,0:T(8,128)(2,1)}, u32[]{:S(2)}, u32[]{:S(2)}) collective-permute-start(bf16[256,1024]{1,0:T(8,128)(2,1)S(1)} %collective-permute-done.6.refs_12_), channel_id=1, source_target_pairs={{0,4},{4,8},{8,12},{12,0},{1,5},{5,9},{9,13},{13,1},{2,6},{6,10},{... | collective-permute-start | bytes 1572872 | tf_op jit(solution)/shard_map/ppermute | solution.py:34
  156.6 11.7 %collective-permute-start.28 = (bf16[3,32,1024]{2,1,0:T(8,128)(2,1)S(1)}, bf16[3,32,1024]{2,1,0:T(8,128)(2,1)S(1)}, u32[]{:S(2)}, u32[]{:S(2)}) collective-permute-start(bf16[3,32,1024]{2,1,0:T(8,128)(2,1)S(1)} %get-tuple-element.79), channel_id=1, source_target_pairs={{0,32},{32,0},{64,96},{96,64},{1,33},{33,1},{65,97},{97,65},{2,34}... | collective-permute-start | bytes 589832 | tf_op jit(solution)/shard_map/ppermute | solution.py:43
  159.2 9.1 %collective-permute-start.29 = (bf16[3,32,1024]{2,1,0:T(8,128)(2,1)S(1)}, bf16[3,32,1024]{2,1,0:T(8,128)(2,1)S(1)}, u32[]{:S(2)}, u32[]{:S(2)}) collective-permute-start(bf16[3,32,1024]{2,1,0:T(8,128)(2,1)S(1)} %get-tuple-element.80), channel_id=1, source_target_pairs={{0,96},{32,64},{64,0},{96,32},{1,97},{33,65},{65,1},{97,33},{2,98}... | collective-permute-start | bytes 589832 | tf_op jit(solution)/shard_map/ppermute | solution.py:43
  160.8 16.3 %collective-permute-start.48 = (bf16[256,1024]{1,0:T(8,128)(2,1)S(1)}, bf16[256,1024]{1,0:T(8,128)(2,1)S(1)}, u32[]{:S(2)}, u32[]{:S(2)}) collective-permute-start(bf16[256,1024]{1,0:T(8,128)(2,1)S(1)} %collective-permute-done.6.refs_12_), channel_id=1, source_target_pairs={{0,8},{4,12},{8,0},{12,4},{1,9},{5,13},{9,1},{13,5},{2,10},{6,14},... | collective-permute-start | bytes 1572872 | tf_op jit(solution)/shard_map/ppermute | solution.py:34
  168.3 14.3 %collective-permute-start.30 = (bf16[128,1024]{1,0:T(8,128)(2,1)S(1)}, bf16[128,1024]{1,0:T(8,128)(2,1)S(1)}, u32[]{:S(2)}, u32[]{:S(2)}) collective-permute-start(bf16[128,1024]{1,0:T(8,128)(2,1)S(1)} %maximum_bitcast_fusion.refs_4_), channel_id=1, source_target_pairs={{0,4},{4,8},{8,12},{12,0},{1,5},{5,9},{9,13},{13,1},{2,6},{6,10},{... | collective-permute-start | bytes 786440 | tf_op jit(solution)/shard_map/ppermute | solution.py:34
  169.6 17.1 %collective-permute-start.31 = (bf16[128,1024]{1,0:T(8,128)(2,1)S(1)}, bf16[128,1024]{1,0:T(8,128)(2,1)S(1)}, u32[]{:S(2)}, u32[]{:S(2)}) collective-permute-start(bf16[128,1024]{1,0:T(8,128)(2,1)S(1)} %maximum_bitcast_fusion.refs_4_), channel_id=1, source_target_pairs={{0,8},{4,12},{8,0},{12,4},{1,9},{5,13},{9,1},{13,5},{2,10},{6,14},... | collective-permute-start | bytes 786440 | tf_op jit(solution)/shard_map/ppermute | solution.py:34
  172.1 24.9 %collective-permute-start.40 = (bf16[2,128,1024]{2,1,0:T(8,128)(2,1)S(1)}, bf16[2,128,1024]{2,1,0:T(8,128)(2,1)S(1)}, u32[]{:S(2)}, u32[]{:S(2)}) collective-permute-start(bf16[2,128,1024]{2,1,0:T(8,128)(2,1)S(1)} %pad_maximum_fusion.1.refs_4_), channel_id=1, source_target_pairs={{0,1},{1,2},{2,3},{3,0},{4,5},{5,6},{6,7},{7,4},{8,9},{9,10},{10,1... | collective-permute-start | bytes 1572872 | tf_op jit(solution)/shard_map/ppermute | solution.py:34
  172.6 24.5 %collective-permute-start.41 = (bf16[2,128,1024]{2,1,0:T(8,128)(2,1)S(1)}, bf16[2,128,1024]{2,1,0:T(8,128)(2,1)}, u32[]{:S(2)}, u32[]{:S(2)}) collective-permute-start(bf16[2,128,1024]{2,1,0:T(8,128)(2,1)S(1)} %pad_maximum_fusion.1.refs_4_), channel_id=1, source_target_pairs={{0,2},{1,3},{2,0},{3,1},{4,6},{5,7},{6,4},{7,5},{8,10},{9,11},{10,... | collective-permute-start | bytes 1572872 | tf_op jit(solution)/shard_map/ppermute | solution.py:34
  177.1 20.7 %collective-permute-start.42 = (bf16[2,128,1024]{2,1,0:T(8,128)(2,1)S(1)}, bf16[2,128,1024]{2,1,0:T(8,128)(2,1)}, u32[]{:S(2)}, u32[]{:S(2)}) collective-permute-start(bf16[2,128,1024]{2,1,0:T(8,128)(2,1)S(1)} %pad_maximum_fusion.1.refs_4_), channel_id=1, source_target_pairs={{0,3},{1,0},{2,1},{3,2},{4,7},{5,4},{6,5},{7,6},{8,11},{9,8},{10,9... | collective-permute-start | bytes 1572872 | tf_op jit(solution)/shard_map/ppermute | solution.py:34
  190.8 16.4 %collective-permute-start.49 = (bf16[256,1024]{1,0:T(8,128)(2,1)S(1)}, bf16[256,1024]{1,0:T(8,128)(2,1)S(1)}, u32[]{:S(2)}, u32[]{:S(2)}) collective-permute-start(bf16[256,1024]{1,0:T(8,128)(2,1)S(1)} %collective-permute-done.6.refs_12_), channel_id=1, source_target_pairs={{0,12},{4,0},{8,4},{12,8},{1,13},{5,1},{9,5},{13,9},{2,14},{6,2},{... | collective-permute-start | bytes 1572872 | tf_op jit(solution)/shard_map/ppermute | solution.py:34
  197.8 11.8 %collective-permute-start.43 = (bf16[2,128,1024]{2,1,0:T(8,128)(2,1)S(1)}, bf16[2,128,1024]{2,1,0:T(8,128)(2,1)S(1)}, u32[]{:S(2)}, u32[]{:S(2)}) collective-permute-start(bf16[2,128,1024]{2,1,0:T(8,128)(2,1)S(1)} %pad_maximum_fusion.1.refs_4_), channel_id=1, source_target_pairs={{0,16},{16,0},{1,17},{17,1},{2,18},{18,2},{3,19},{19,3},{4,20},{20... | collective-permute-start | bytes 1572872 | tf_op jit(solution)/shard_map/ppermute | solution.py:34
  197.8 12.1 %collective-permute-start.44 = (bf16[2,128,1024]{2,1,0:T(8,128)(2,1)S(1)}, bf16[2,128,1024]{2,1,0:T(8,128)(2,1)}, u32[]{:S(2)}, u32[]{:S(2)}) collective-permute-start(bf16[2,128,1024]{2,1,0:T(8,128)(2,1)S(1)} %collective-permute-done.40.refs_5_), channel_id=1, source_target_pairs={{0,16},{16,0},{1,17},{17,1},{2,18},{18,2},{3,19},{19,3},{4,20},{20... | collective-permute-start | bytes 1572872 | tf_op jit(solution)/shard_map/ppermute | solution.py:34
  198.6 12.3 %collective-permute-start.45 = (bf16[2,128,1024]{2,1,0:T(8,128)(2,1)}, bf16[2,128,1024]{2,1,0:T(8,128)(2,1)}, u32[]{:S(2)}, u32[]{:S(2)}) collective-permute-start(bf16[2,128,1024]{2,1,0:T(8,128)(2,1)} %collective-permute-done.41.refs_6_), channel_id=1, source_target_pairs={{0,16},{16,0},{1,17},{17,1},{2,18},{18,2},{3,19},{19,3},{4,20},{20... | collective-permute-start | bytes 1572872 | tf_op jit(solution)/shard_map/ppermute | solution.py:34
  200.0 10.9 %collective-permute-start.46 = (bf16[2,128,1024]{2,1,0:T(8,128)(2,1)}, bf16[2,128,1024]{2,1,0:T(8,128)(2,1)}, u32[]{:S(2)}, u32[]{:S(2)}) collective-permute-start(bf16[2,128,1024]{2,1,0:T(8,128)(2,1)} %collective-permute-done.42.refs_7_), channel_id=1, source_target_pairs={{0,16},{16,0},{1,17},{17,1},{2,18},{18,2},{3,19},{19,3},{4,20},{20... | collective-permute-start | bytes 1572872 | tf_op jit(solution)/shard_map/ppermute | solution.py:34
  207.2 25.8 %collective-permute-start.37 = (bf16[256,1024]{1,0:T(8,128)(2,1)}, bf16[256,1024]{1,0:T(8,128)(2,1)S(1)}, u32[]{:S(2)}, u32[]{:S(2)}) collective-permute-start(bf16[256,1024]{1,0:T(8,128)(2,1)} %get-tuple-element.40), channel_id=1, source_target_pairs={{0,3},{1,0},{2,1},{3,2},{4,7},{5,4},{6,5},{7,6},{8,11},{9,8},{10,9... | collective-permute-start | bytes 1572872 | tf_op jit(solution)/shard_map/ppermute | solution.py:34
  209.6 24.0 %collective-permute-start.38 = (bf16[256,1024]{1,0:T(8,128)(2,1)}, bf16[256,1024]{1,0:T(8,128)(2,1)S(1)}, u32[]{:S(2)}, u32[]{:S(2)}) collective-permute-start(bf16[256,1024]{1,0:T(8,128)(2,1)} %get-tuple-element.41), channel_id=1, source_target_pairs={{0,2},{1,3},{2,0},{3,1},{4,6},{5,7},{6,4},{7,5},{8,10},{9,11},{10,... | collective-permute-start | bytes 1572872 | tf_op jit(solution)/shard_map/ppermute | solution.py:34
  210.4 26.2 %collective-permute-start.39 = (bf16[256,1024]{1,0:T(8,128)(2,1)}, bf16[256,1024]{1,0:T(8,128)(2,1)S(1)}, u32[]{:S(2)}, u32[]{:S(2)}) collective-permute-start(bf16[256,1024]{1,0:T(8,128)(2,1)} %get-tuple-element.42), channel_id=1, source_target_pairs={{0,1},{1,2},{2,3},{3,0},{4,5},{5,6},{6,7},{7,4},{8,9},{9,10},{10,1... | collective-permute-start | bytes 1572872 | tf_op jit(solution)/shard_map/ppermute | solution.py:34
  225.6 15.1 %collective-permute-start.50 = (bf16[256,1024]{1,0:T(8,128)(2,1)}, bf16[256,1024]{1,0:T(8,128)(2,1)S(1)}, u32[]{:S(2)}, u32[]{:S(2)}) collective-permute-start(bf16[256,1024]{1,0:T(8,128)(2,1)} %get-tuple-element.44), channel_id=1, source_target_pairs={{0,12},{4,0},{8,4},{12,8},{1,13},{5,1},{9,5},{13,9},{2,14},{6,2},{... | collective-permute-start | bytes 1572872 | tf_op jit(solution)/shard_map/ppermute | solution.py:34
  226.7 16.6 %collective-permute-start.51 = (bf16[256,1024]{1,0:T(8,128)(2,1)}, bf16[256,1024]{1,0:T(8,128)(2,1)S(1)}, u32[]{:S(2)}, u32[]{:S(2)}) collective-permute-start(bf16[256,1024]{1,0:T(8,128)(2,1)} %get-tuple-element.45), channel_id=1, source_target_pairs={{0,8},{4,12},{8,0},{12,4},{1,9},{5,13},{9,1},{13,5},{2,10},{6,14},... | collective-permute-start | bytes 1572872 | tf_op jit(solution)/shard_map/ppermute | solution.py:34
  233.0 20.1 %collective-permute-start.52 = (bf16[256,1024]{1,0:T(8,128)(2,1)}, bf16[256,1024]{1,0:T(8,128)(2,1)S(1)}, u32[]{:S(2)}, u32[]{:S(2)}) collective-permute-start(bf16[256,1024]{1,0:T(8,128)(2,1)} %get-tuple-element.46), channel_id=1, source_target_pairs={{0,4},{4,8},{8,12},{12,0},{1,5},{5,9},{9,13},{13,1},{2,6},{6,10},{... | collective-permute-start | bytes 1572872 | tf_op jit(solution)/shard_map/ppermute | solution.py:34
  (32 other events, 504.0 us)
Sparse Core Ops, SparseCore 0:
  110.7 40.2 all-gather.1
